TPU v7x, 128 devices: a whole 4x4x4 slice. The times are simulated.
128 devices in a mesh: blk: 16 (over x, z), order: 8 (over y, core).
Axes of the slice: x: 4, y: 4, z: 4, core: 2. Of those that a mesh axis runs over, the one named last changes fastest.
Arguments:
- field: float32 [16, 1024, 4096], P(None, 'blk', 'order'), may hold values from -6 to 6
- ocean_mask: int32 [1024, 4096], P('blk', 'order'), may hold values from 0 to 1, as said below
- plan: int32 [1024], replicated, may hold values from 0 to 768, as said below
- legendre: bfloat16 [768, 1024, 1024], P('blk', 'order'), may hold values from -0.3125 to 0.3125
Outputs:
- coefficients: float32 [1024, 16, 2, 1024], P('blk', None, None, 'order')
Inputs may be any that keep to these rules, and one draw needn't show every extreme that they name: `ocean_mask`: exactly 256 cycles are all land, at the ends of the cycle order; every other cycle has an ocean point. plan is 768 exactly at the cycles that are all land, and names every slot below 768 once at the other cycles; slot p belongs to index p // 48 of blk; the cycles of one index of blk name at most 4 slots of one index, and in every draw some index of blk names exactly 4 slots of some index.
All inputs are finite; a program needn't handle non-finite values.
Results may differ from a plain program's by a relative error of at most 0.0029.
Values may be sent and summed in bfloat16 or wider, within the bound.
A program may use at most 128 MiB of HBM per device.

v0:
```python
import math

import jax
import jax.numpy as jnp
from jax import lax
from jax.sharding import PartitionSpec as P

NLON = 4096
M = 1024


def twiddle(first, count):
    longitudes = first + jnp.arange(count, dtype=jnp.int32)
    orders = jnp.arange(M, dtype=jnp.int32)
    product = longitudes[:, None] * orders[None, :] % NLON
    angle = product.astype(jnp.float32) * (2.0 * math.pi / NLON)
    scale = 1.0 / math.sqrt(NLON)
    return jnp.stack([jnp.cos(angle) * scale, -jnp.sin(angle) * scale], axis=1)


def transform(values, table):
    return jnp.einsum("frn,ncm->frcm", values, table, precision=lax.Precision.HIGHEST)


def pack_cycles(masked, plan, slot_dev):
    n_blk = lax.axis_size("blk")
    own_index = lax.axis_index("blk")
    cycle_dev = masked.shape[1]
    cap = (cycle_dev + n_blk - 1) // n_blk
    grid = plan.reshape(n_blk, cycle_dev)
    owner = grid // slot_dev
    positions = jnp.arange(cycle_dev, dtype=jnp.int32)
    earlier = positions[None, :] < positions[:, None]
    same_owner = owner[:, :, None] == owner[:, None, :]
    rank = jnp.sum(same_owner & earlier[None], axis=2, dtype=jnp.int32)
    send_pos = owner * cap + rank
    local_pos = lax.dynamic_index_in_dim(send_pos, own_index, 0, keepdims=False)
    buffer_ids = jnp.arange(n_blk * cap, dtype=jnp.int32)
    send_onehot = (buffer_ids[:, None] == local_pos[None, :]).astype(jnp.float32)
    outgoing = jnp.einsum("qr,frn->fqn", send_onehot, masked, precision=lax.Precision.HIGHEST)
    arrived = lax.all_to_all(outgoing, "blk", split_axis=1, concat_axis=1, tiled=True)
    source_pos = (jnp.arange(n_blk, dtype=jnp.int32)[:, None] * cap + rank).reshape(-1)
    mine = (owner == own_index).reshape(-1)
    slot_local = (grid % slot_dev).reshape(-1)
    slot_ids = jnp.arange(slot_dev, dtype=jnp.int32)
    slot_onehot = ((slot_local[None, :] == slot_ids[:, None]) & mine[None, :]).astype(jnp.float32)
    source_onehot = (source_pos[:, None] == buffer_ids[None, :]).astype(jnp.float32)
    receive_map = jnp.dot(slot_onehot, source_onehot, precision=lax.Precision.HIGHEST)
    return jnp.einsum("pq,fqn->fpn", receive_map, arrived, precision=lax.Precision.HIGHEST)


def body(field, ocean_mask, plan, legendre):
    lon_local = field.shape[2]
    slot_dev = legendre.shape[0]
    masked = field * ocean_mask.astype(jnp.float32)[None]
    packed = pack_cycles(masked, plan, slot_dev)
    first = lax.axis_index("order") * lon_local
    terms = transform(packed, twiddle(first, lon_local))
    spectrum = lax.psum_scatter(terms, "order", scatter_dimension=3, tiled=True).astype(
        jnp.bfloat16
    )
    terms = jnp.einsum("pml,fpcm->lfcm", legendre, spectrum, preferred_element_type=jnp.float32)
    coefficients = lax.psum_scatter(terms, "blk", scatter_dimension=0, tiled=True)
    return coefficients


def solution(mesh):
    placed = (P(None, "blk", "order"), P("blk", "order"), P(), P("blk", "order", None))
    return jax.shard_map(
        body, mesh=mesh, in_specs=placed, out_specs=P("blk", None, None, "order"), check_vma=False
    )
```

profile of v0, /device:TPU:0, one launch (start us, length us, event | category | flops | bytes accessed | tf_op | source)
XLA Modules:
  0.0 277.7 jit_solution(17178055627215693072)
XLA Ops:
  6.6 0.7 add_select_fusion.3
  7.3 0.7 fusion.31
  8.0 0.1 and.67
  8.0 0.1 div.20
  8.1 0.9 convert_element_type.26
  9.0 0.5 convert_reduce_fusion
  9.6 3.0 %fusion.18 = f32[16,64,512]{2,1,0:T(8,128)S(1)} fusion(f32[16,64,512]{2,1,0:T(8,128)} %param.4, f32[64,512]{1,0:T(8,128)S(1)} %convert_element_type.26, s32[64]{0:T(128)S(1)} %fusion.33), kind=kOutput, calls=%fused_computation.22 | convolution fusion | flops 403181568 | bytes 4325632 | tf_op jit(solution)/shard_map/qr,frn->fqn/dot_general | solution.py:40
  12.6 2.5 copy.10
  15.1 8.0 %all-to-all-start = ((f32[16,64,512]{2,0,1:T(8,128)}), f32[16,64,512]{2,0,1:T(8,128)S(1)}, u32[]{:S(2)}, u32[]{:S(2)}) async-start(f32[16,64,512]{2,0,1:T(8,128)} %copy.10), calls=%async_computation | async-start | bytes 4194304 | tf_op jit(solution)/shard_map/all_to_all | solution.py:41
  23.1 0.0 reduce-scatter.3.cloned.1.call-start
  23.2 0.1 broadcast_add_fusion
  23.3 0.1 add.77
  23.3 0.3 convolution_bitcast_fusion
  23.7 10.8 %cosine_multiply_fusion = (f32[512,1,1024]{2,0,1:T(8,128)}, f32[512,1,1024]{2,0,1:T(8,128)}) fusion(s32[512]{0:T(512)S(1)} %iota_add_fusion), kind=kLoop, calls=%fused_computation.16 | loop fusion | flops 8912896 | bytes 4196352 | tf_op jit(solution)/shard_map/mul | solution.py:18
  34.4 19.1 %all-to-all-done = f32[16,64,512]{2,0,1:T(8,128)S(1)} async-done(((f32[16,64,512]{2,0,1:T(8,128)}), f32[16,64,512]{2,0,1:T(8,128)S(1)}, u32[]{:S(2)}, u32[]{:S(2)}) %all-to-all-start) | async-done | bytes 2097184 | tf_op jit(solution)/shard_map/all_to_all | solution.py:41
  53.5 0.0 copy-start
  53.5 2.9 %fusion.11 = f32[16,512,48]{1,2,0:T(8,128)S(1)} fusion(f32[48,64,1]{1,0,2:T(8,128)S(1)} %convolution_bitcast_fusion, f32[16,64,512]{2,0,1:T(8,128)S(1)} %all-to-all-done), kind=kOutput, calls=%fused_computation.13 | convolution fusion | flops 301989888 | bytes 3682304 | tf_op jit(solution)/shard_map/pq,fqn->fpn/dot_general | solution.py:49
  56.5 0.0 copy-done
  56.5 13.4 %fusion.5 = f32[16,48,2,1024]{3,1,2,0:T(8,128)} fusion(f32[512,1,1024]{2,0,1:T(8,128)} %get-tuple-element.10, f32[512,1,1024]{2,0,1:T(8,128)S(1)} %copy-done, f32[16,512,48]{1,2,0:T(8,128)S(1)} %fusion.11), kind=kOutput, calls=%fused_computation.4 | convolution fusion | flops 9664724992 | bytes 12058624 | tf_op jit(solution)/shard_map/frn,ncm->frcm/dot_general | solution.py:22
  69.8 0.0 reduce-scatter.3.cloned.1.call-update
  69.9 0.2 reduce-scatter.5.cloned.1.call-start
  70.1 40.5 %reduce-scatter.3.cloned.1.call-done = f32[16,48,2,128]{3,1,2,0:T(8,128)} async-done(((f32[16,48,2,1024]{3,1,2,0:T(8,128)}), f32[16,48,2,128]{3,1,2,0:T(8,128)}) %reduce-scatter.3.cloned.1.call-update) | async-done | bytes 786448 | tf_op jit(solution)/shard_map/reduce_scatter | solution.py:59
  110.6 1.2 convert_element_type.29
  111.8 1.4 copy.12
  113.2 26.5 %fusion.2 = f32[1024,16,2,128]{0,1,2,3:T(8,128)} fusion(bf16[16,48,2,128]{1,0,2,3:T(8,128)(2,1)S(1)} %copy.12, bf16[48,128,1024,1]{2,1,0,3:T(8,128)(2,1)} %bitcast.24), kind=kOutput, calls=%fused_computation.2 | convolution fusion | flops 402653184 | bytes 29753344 | tf_op jit(solution)/shard_map/pml,fpcm->lfcm/dot_general | solution.py:62
  139.7 17.5 %copy.14 = f32[1024,16,2,128]{3,1,2,0:T(8,128)} copy(f32[1024,16,2,128]{0,1,2,3:T(8,128)} %fusion.2) | data formatting | bytes 33554432 | tf_op jit(solution)/shard_map/pml,fpcm->lfcm/transpose | solution.py:62
  157.2 0.0 reduce-scatter.5.cloned.1.call-update
  157.2 110.9 %reduce-scatter.5.cloned.1.call-done = f32[64,16,2,128]{3,1,2,0:T(8,128)} async-done(((f32[1024,16,2,128]{3,1,2,0:T(8,128)}), f32[64,16,2,128]{3,1,2,0:T(8,128)}) %reduce-scatter.5.cloned.1.call-update) | async-done | bytes 1048592 | tf_op jit(solution)/shard_map/reduce_scatter | solution.py:63
  268.1 2.7 copy.15
  (5 shorter events, 0.0 us)
Async XLA Ops:
  15.1 38.4 %all-to-all-start = ((f32[16,64,512]{2,0,1:T(8,128)}), f32[16,64,512]{2,0,1:T(8,128)S(1)}, u32[]{:S(2)}, u32[]{:S(2)}) async-start(f32[16,64,512]{2,0,1:T(8,128)} %copy.10), calls=%async_computation | async-start | bytes 4194304 | tf_op jit(solution)/shard_map/all_to_all | solution.py:41
  23.1 87.5 %reduce-scatter.3.cloned.1.call-start = ((), (), s32[]{:S(2)}) async-start(), calls=%async_computation.3 | async-start | bytes 7077888 | tf_op jit(solution)/shard_map/reduce_scatter | solution.py:59
  53.5 3.0 %copy-start = (f32[512,1,1024]{2,0,1:T(8,128)S(1)}, f32[512,1,1024]{2,0,1:T(8,128)}, u32[]{:S(2)}) copy-start(f32[512,1,1024]{2,0,1:T(8,128)} %get-tuple-element.9) | copy-start | bytes 6291460
  69.9 198.2 %reduce-scatter.5.cloned.1.call-start = ((), (), s32[]{:S(2)}) async-start(), calls=%async_computation.4 | async-start | bytes 17825792 | tf_op jit(solution)/shard_map/reduce_scatter | solution.py:63
Sparse Core Ops, SparseCore 0:
  70.0 40.5 reduce-scatter.2
  157.4 110.6 reduce-scatter.4
where the time goes:
time: 279 us; the launch traced here: 278 us
  waiting for transfers between devices  170 us (61%)
  matrix products  46.1 us (17%)
  local copies, waits for them, and re-layouts  24.4 us (9%)
  other arithmetic  14.9 us (5%)
  between operations  13.5 us (5%)
  starting transfers between devices  8.25 us (3%)
    reduce_scatter x1, waiting for transfers between devices, body(): lax.psum_scatter(terms, 'blk', scatter_dimension=0, tiled=True)  111 us
    reduce_scatter x1, waiting for transfers between devices, body(): lax.psum_scatter(terms, 'order', scatter_dimension=3, tiled=True)  40.5 us
    dot_general x1, matrix products, body(): jnp.einsum('pml,fpcm->lfcm', legendre, spectrum, preferred_element_type=j...  26.5 us
    all_to_all x1, waiting for transfers between devices, pack_cycles(): lax.all_to_all(outgoing, 'blk', split_axis=1, concat_axis=1, tiled=True)  19.1 us
    transpose x1, local copies, waits for them, and re-layouts, body(): jnp.einsum('pml,fpcm->lfcm', legendre, spectrum, preferred_element_type=j...  17.5 us
    dot_general x1, matrix products, transform(): jnp.einsum('frn,ncm->frcm', values, table, precision=lax.Precision.HIGHEST)  13.4 us
    mul x1, other arithmetic, twiddle(): return jnp.stack([jnp.cos(angle) * scale, -jnp.sin(angle) * scale], axis=1)  10.8 us
    all_to_all x1, starting transfers between devices, pack_cycles(): lax.all_to_all(outgoing, 'blk', split_axis=1, concat_axis=1, tiled=True)  7.99 us
  transfers between devices with their start and end apart: 3, of which 3 were waited for; matrix products, arithmetic and copies ran while one was open for 4% of the time, Pallas kernels for 0%

commit v1 on v0

--- a/solution.py
+++ b/solution.py
@@ -3,6 +3,8 @@
 import jax
 import jax.numpy as jnp
 from jax import lax
+from jax.experimental import pallas as pl
+from jax.experimental.pallas import tpu as pltpu
 from jax.sharding import PartitionSpec as P
 
 NLON = 4096
@@ -49,6 +51,189 @@
     return jnp.einsum("pq,fqn->fpn", receive_map, arrived, precision=lax.Precision.HIGHEST)
 
 
+MESH = pl.DeviceIdType.MESH
+BF = jnp.bfloat16
+F32 = jnp.float32
+NBLOCK = 8
+
+
+def contract_kernel(spec_ref, e_ref, leg_hbm, out_ref, leg, q, q2, ms1, mr1, ss1, sr1, ms2, mr2, ss2, sr2,
+                    leg_sem, s_sem, r_sem):
+    me = lax.axis_index("blk")
+    x = me // 4
+    z = me % 4
+    for t in range(8):
+        pltpu.make_async_copy(leg_hbm.at[:, pl.ds(16 * t, 16), :], leg.at[t], leg_sem.at[t]).start()
+    barrier = pltpu.get_barrier_semaphore()
+    for nx, nz in ((1, 0), (3, 0), (0, 1), (0, 3)):
+        pl.semaphore_signal(barrier, inc=1, device_id={"blk": (x + nx) % 4 * 4 + (z + nz) % 4}, device_id_type=MESH)
+    pl.semaphore_wait(barrier, 4)
+
+    rows = lax.broadcasted_iota(jnp.int32, (256, 768), 0) % 16
+    lanes = lax.broadcasted_iota(jnp.int32, (256, 768), 1) % 16
+    mask = rows == lanes
+    low = lax.broadcasted_iota(jnp.int32, (256, 128), 1) < 64
+
+    def neighbour(axis, step):
+        nx = (x + step * (1 - axis)) % 4
+        nz = (z + step * axis) % 4
+        return {"blk": nx * 4 + nz}
+
+    def copies(s, kind, src, dst, axis):
+        minus = pltpu.make_async_remote_copy(
+            src_ref=src.at[s, 0], dst_ref=dst.at[s, 0], send_sem=s_sem.at[s, kind, 0], recv_sem=r_sem.at[s, kind, 0],
+            device_id=neighbour(axis, 3), device_id_type=MESH)
+        plus = pltpu.make_async_remote_copy(
+            src_ref=src.at[s, 1], dst_ref=dst.at[s, 1], send_sem=s_sem.at[s, kind, 1], recv_sem=r_sem.at[s, kind, 1],
+            device_id=neighbour(axis, 1), device_id_type=MESH)
+        return minus, plus
+
+    A, B = pl.ds(0, 128), pl.ds(128, 128)
+
+    def compute(s):
+        tt = s // 2
+        par = s % 2
+        qs = s % 4
+
+        @pl.when(par == 0)
+        def _():
+            for h in (0, 1):
+                t = tt + 4 * h
+                pltpu.make_async_copy(leg_hbm.at[:, pl.ds(16 * t, 16), :], leg.at[t], leg_sem.at[t]).wait()
+
+        lhs = []
+        for h in (0, 1):
+            sp = spec_ref[tt + 4 * h, pl.ds(16 * par, 16)]
+            sp = sp.reshape(256, sp.shape[-1])
+            ex = jnp.dot(sp, e_ref[...], preferred_element_type=F32)
+            lhs.append(jnp.where(mask, ex, 0.0).astype(BF))
+        for bx in range(4):
+            pa, pb = [
+                jnp.dot(lhs[h], leg[tt + 4 * h, :, :, 256 * bx:256 * bx + 256].reshape(768, 256),
+                        preferred_element_type=F32)
+                for h in (0, 1)
+            ]
+            for half in range(2):
+                a = pa[:, 128 * half:128 * half + 128]
+                b = pb[:, 128 * half:128 * half + 128]
+                first = jnp.where(low, a, pltpu.roll(b, 64, 1))
+                second = jnp.where(low, pltpu.roll(a, 64, 1), b)
+                for bz, value in ((2 * half, first), (2 * half + 1, second)):
+                    q[qs, bx * (1 - par) + bz * par, bz * (1 - par) + bx * par] = value
+        i = x * (1 - par) + z * par
+        c1, c2, c3 = (i + 1) % 4, (i + 2) % 4, (i + 3) % 4
+        ms1[s, 0, 0] = q[qs, c2, :, A, :].astype(BF)
+        ms1[s, 0, 1] = q[qs, c3, :, B, :].astype(BF)
+        ms1[s, 1, 0] = q[qs, c2, :, B, :].astype(BF)
+        ms1[s, 1, 1] = q[qs, c1, :, A, :].astype(BF)
+        for c in copies(s, 0, ms1, mr1, par):
+            c.start()
+
+    def relay1(s):
+        par = s % 2
+        qs = s % 4
+        i = x * (1 - par) + z * par
+        c1, c3 = (i + 1) % 4, (i + 3) % 4
+        minus, plus = copies(s, 0, ms1, mr1, par)
+        send = copies(s, 1, ss1, sr1, par)
+        minus.wait_recv()
+        ss1[s, 0] = (q[qs, c3, :, A, :] + mr1[s, 0, 0].astype(F32)).astype(BF)
+        send[0].start()
+        plus.wait_recv()
+        ss1[s, 1] = (q[qs, c1, :, B, :] + mr1[s, 1, 0].astype(F32)).astype(BF)
+        send[1].start()
+
+    def owner1(s):
+        par = s % 2
+        qs = s % 4
+        i = x * (1 - par) + z * par
+        minus, plus = copies(s, 1, ss1, sr1, par)
+        minus.wait_recv()
+        q2[s, :, A, :] = q[qs, i, :, A, :] + mr1[s, 1, 1].astype(F32) + sr1[s, 0].astype(F32)
+        plus.wait_recv()
+        q2[s, :, B, :] = q[qs, i, :, B, :] + mr1[s, 0, 1].astype(F32) + sr1[s, 1].astype(F32)
+        j = z * (1 - par) + x * par
+        d1, d2, d3 = (j + 1) % 4, (j + 2) % 4, (j + 3) % 4
+        ms2[s, 0, 0] = q2[s, d2, A, :].astype(BF)
+        ms2[s, 0, 1] = q2[s, d3, B, :].astype(BF)
+        ms2[s, 1, 0] = q2[s, d2, B, :].astype(BF)
+        ms2[s, 1, 1] = q2[s, d1, A, :].astype(BF)
+        for c in copies(s, 2, ms2, mr2, 1 - par):
+            c.start()
+
+    def relay2(s):
+        par = s % 2
+        j = z * (1 - par) + x * par
+        d1, d3 = (j + 1) % 4, (j + 3) % 4
+        minus, plus = copies(s, 2, ms2, mr2, 1 - par)
+        send = copies(s, 3, ss2, sr2, 1 - par)
+        minus.wait_recv()
+        ss2[s, 0] = (q2[s, d3, A, :] + mr2[s, 0, 0].astype(F32)).astype(BF)
+        send[0].start()
+        plus.wait_recv()
+        ss2[s, 1] = (q2[s, d1, B, :] + mr2[s, 1, 0].astype(F32)).astype(BF)
+        send[1].start()
+
+    def owner2(s):
+        par = s % 2
+        j = z * (1 - par) + x * par
+        minus, plus = copies(s, 3, ss2, sr2, 1 - par)
+        minus.wait_recv()
+        out_ref[s, A, :] = q2[s, j, A, :] + mr2[s, 1, 1].astype(F32) + sr2[s, 0].astype(F32)
+        plus.wait_recv()
+        out_ref[s, B, :] = q2[s, j, B, :] + mr2[s, 0, 1].astype(F32) + sr2[s, 1].astype(F32)
+
+    stages = ((compute, 0), (relay1, 1), (owner1, 2), (relay2, 3), (owner2, 4))
+
+    def step(k, carry):
+        for stage, lag in stages:
+            @pl.when((k >= lag) & (k < NBLOCK + lag))
+            def _():
+                stage(k - lag)
+        return carry
+
+    lax.fori_loop(0, NBLOCK + stages[-1][1], step, 0)
+
+    def drain(s, carry):
+        par = s % 2
+        for kind, src, dst, axis in ((0, ms1, mr1, par), (1, ss1, sr1, par), (2, ms2, mr2, 1 - par), (3, ss2, sr2, 1 - par)):
+            for c in copies(s, kind, src, dst, axis):
+                c.wait_send()
+        return carry
+
+    lax.fori_loop(0, NBLOCK, drain, 0)
+
+
+def contract(spec, expand, legendre):
+    big = (NBLOCK, 2, 2, 4, 128, 128)
+    small = (NBLOCK, 2, 2, 128, 128)
+    vmem = pl.BlockSpec(memory_space=pltpu.VMEM)
+    return pl.pallas_call(
+        contract_kernel,
+        out_shape=jax.ShapeDtypeStruct((NBLOCK, 256, 128), F32),
+        in_specs=[vmem, vmem, pl.BlockSpec(memory_space=pl.ANY)],
+        out_specs=vmem,
+        scratch_shapes=[
+            pltpu.VMEM((8, 48, 16, 1024), BF),
+            pltpu.VMEM((4, 4, 4, 256, 128), F32),
+            pltpu.VMEM((NBLOCK, 4, 256, 128), F32),
+            pltpu.VMEM(big, BF), pltpu.VMEM(big, BF),
+            pltpu.VMEM((NBLOCK, 2, 4, 128, 128), BF), pltpu.VMEM((NBLOCK, 2, 4, 128, 128), BF),
+            pltpu.VMEM(small, BF), pltpu.VMEM(small, BF),
+            pltpu.VMEM((NBLOCK, 2, 128, 128), BF), pltpu.VMEM((NBLOCK, 2, 128, 128), BF),
+            pltpu.SemaphoreType.DMA((8,)),
+            pltpu.SemaphoreType.DMA((NBLOCK, 4, 2)),
+            pltpu.SemaphoreType.DMA((NBLOCK, 4, 2)),
+        ],
+        compiler_params=pltpu.CompilerParams(collective_id=0, has_side_effects=True, vmem_limit_bytes=60 * 2**20),
+    )(spec, expand, legendre)
+
+
+def finish(blocks):
+    blocks = blocks.reshape(4, 2, 16, 16, 2, 64)
+    return jnp.transpose(blocks, (5, 1, 2, 4, 0, 3)).reshape(64, 16, 2, 128)
+
+
 def body(field, ocean_mask, plan, legendre):
     lon_local = field.shape[2]
     slot_dev = legendre.shape[0]
@@ -59,9 +244,10 @@
     spectrum = lax.psum_scatter(terms, "order", scatter_dimension=3, tiled=True).astype(
         jnp.bfloat16
     )
-    terms = jnp.einsum("pml,fpcm->lfcm", legendre, spectrum, preferred_element_type=jnp.float32)
-    coefficients = lax.psum_scatter(terms, "blk", scatter_dimension=0, tiled=True)
-    return coefficients
+    spec = spectrum.reshape(16, 48, 2, 8, 16).transpose(3, 0, 2, 4, 1).reshape(8, 32, 16, 48)
+    slots = jnp.arange(48, dtype=jnp.int32)[:, None]
+    expand = (slots == jnp.arange(768, dtype=jnp.int32)[None, :] // 16).astype(BF)
+    return finish(contract(spec, expand, legendre))
 
 
 def solution(mesh):

time: 279 us -> 195 us (0.70)
  waiting for transfers between devices: 170 us -> 59 us
  Pallas kernels: 0 us -> 67.1 us
  matrix products: 46.1 us -> 19.6 us
  local copies, waits for them, and re-layouts: 24.4 us -> 11.3 us
    reduce_scatter x1 -> x0, waiting for transfers between devices: 111 us -> none  [body(): lax.psum_scatter(terms, 'blk', scatter_dimension=0, tiled=True)]
    pallas_call x0 -> x1, Pallas kernels: none -> 67.1 us  [contract(): pl.pallas_call(contract_kernel, out_shape=jax.ShapeDtypeStruct((NBLOCK, 2...]
    dot_general x1 -> x0, matrix products: 26.5 us -> none  [body(): jnp.einsum('pml,fpcm->lfcm', legendre, spectrum, preferred_element_type=j...]
    transpose x1, local copies, waits for them, and re-layouts: 17.5 us -> 1.18 us  [body(): spectrum.reshape(16, 48, 2, 8, 16).transpose(3, 0, 2, 4, 1)]
    reshape x0 -> x3, local copies, waits for them, and re-layouts: none -> 6.83 us  [the longest x2 4.11 us: finish(): blocks = blocks.reshape(4, 2, 16, 16, 2, 64)]
  transfers between devices with their start and end apart: 3 -> 2, of which waited for: 3 -> 2; matrix products, arithmetic and copies ran while one was open for 4% -> 6% of each run, Pallas kernels for 0% -> 0%
where the time goes in v1:
time: 195 us; the launch traced here: 194 us
  Pallas kernels  67.1 us (34%)
  waiting for transfers between devices  59 us (30%)
  matrix products  19.6 us (10%)
  other arithmetic  15.5 us (8%)
  between operations  13.5 us (7%)
  local copies, waits for them, and re-layouts  11.3 us (6%)
  starting transfers between devices  8.21 us (4%)
    pallas_call x1, Pallas kernels, contract(): pl.pallas_call(contract_kernel, out_shape=jax.ShapeDtypeStruct((NBLOCK, 2...  67.1 us
    reduce_scatter x1, waiting for transfers between devices, body(): lax.psum_scatter(terms, 'order', scatter_dimension=3, tiled=True)  40.1 us
    all_to_all x1, waiting for transfers between devices, pack_cycles(): lax.all_to_all(outgoing, 'blk', split_axis=1, concat_axis=1, tiled=True)  18.9 us
    dot_general x1, matrix products, transform(): jnp.einsum('frn,ncm->frcm', values, table, precision=lax.Precision.HIGHEST)  13.4 us
    mul x1, other arithmetic, twiddle(): return jnp.stack([jnp.cos(angle) * scale, -jnp.sin(angle) * scale], axis=1)  10.8 us
    all_to_all x1, starting transfers between devices, pack_cycles(): lax.all_to_all(outgoing, 'blk', split_axis=1, concat_axis=1, tiled=True)  7.99 us
    reshape x2, local copies, waits for them, and re-layouts, finish(): blocks = blocks.reshape(4, 2, 16, 16, 2, 64)  4.11 us
  transfers between devices with their start and end apart: 2, of which 2 were waited for; matrix products, arithmetic and copies ran while one was open for 6% of the time, Pallas kernels for 0%

profile of v1, /device:TPU:0, one launch (start us, length us, event | category | flops | bytes accessed | tf_op | source)
XLA Modules:
  0.0 194.3 jit_solution(6198814179122840624)
XLA Ops:
  6.6 0.7 add_select_fusion.4
  7.3 0.7 fusion.27
  8.0 0.1 and.82
  8.0 0.1 div.28
  8.1 0.9 convert_element_type.29
  9.0 0.5 convert_reduce_fusion
  9.6 3.0 %fusion.13 = f32[16,64,512]{2,1,0:T(8,128)S(1)} fusion(f32[16,64,512]{2,1,0:T(8,128)} %param.4, f32[64,512]{1,0:T(8,128)S(1)} %convert_element_type.29, s32[64]{0:T(128)S(1)} %fusion.32), kind=kOutput, calls=%fused_computation.19 | convolution fusion | flops 403181568 | bytes 4325632 | tf_op jit(solution)/shard_map/qr,frn->fqn/dot_general | solution.py:42
  12.6 2.5 %copy.17 = f32[16,64,512]{2,0,1:T(8,128)} copy(f32[16,64,512]{2,1,0:T(8,128)S(1)} %fusion.13) | data formatting | bytes 4194304 | tf_op jit(solution)/shard_map/qr,frn->fqn/transpose | solution.py:42
  15.1 8.0 %all-to-all-start = ((f32[16,64,512]{2,0,1:T(8,128)}), f32[16,64,512]{2,0,1:T(8,128)S(1)}, u32[]{:S(2)}, u32[]{:S(2)}) async-start(f32[16,64,512]{2,0,1:T(8,128)} %copy.17), calls=%async_computation | async-start | bytes 4194304 | tf_op jit(solution)/shard_map/all_to_all | solution.py:43
  23.1 0.2 reduce-scatter.2.cloned.1.call-start
  23.4 0.1 broadcast_add_fusion
  23.4 0.1 add.81
  23.5 0.3 convolution_bitcast_fusion
  23.8 10.8 %cosine_multiply_fusion = (f32[512,1,1024]{2,0,1:T(8,128)}, f32[512,1,1024]{2,0,1:T(8,128)}) fusion(s32[512]{0:T(512)S(1)} %iota_add_fusion), kind=kLoop, calls=%fused_computation.13 | loop fusion | flops 8912896 | bytes 4196352 | tf_op jit(solution)/shard_map/mul | solution.py:20
  34.6 18.9 %all-to-all-done = f32[16,64,512]{2,0,1:T(8,128)S(1)} async-done(((f32[16,64,512]{2,0,1:T(8,128)}), f32[16,64,512]{2,0,1:T(8,128)S(1)}, u32[]{:S(2)}, u32[]{:S(2)}) %all-to-all-start) | async-done | bytes 2097184 | tf_op jit(solution)/shard_map/all_to_all | solution.py:43
  53.5 0.0 copy-start
  53.5 2.9 %fusion.6 = f32[16,512,48]{1,2,0:T(8,128)S(1)} fusion(f32[48,64,1]{1,0,2:T(8,128)S(1)} %convolution_bitcast_fusion, f32[16,64,512]{2,0,1:T(8,128)S(1)} %all-to-all-done), kind=kOutput, calls=%fused_computation.10 | convolution fusion | flops 301989888 | bytes 3682304 | tf_op jit(solution)/shard_map/pq,fqn->fpn/dot_general | solution.py:51
  56.5 0.0 copy-done
  56.5 13.4 %fusion = f32[16,48,2,1024]{3,1,2,0:T(8,128)} fusion(f32[512,1,1024]{2,0,1:T(8,128)} %get-tuple-element.10, f32[512,1,1024]{2,0,1:T(8,128)S(1)} %copy-done, f32[16,512,48]{1,2,0:T(8,128)S(1)} %fusion.6), kind=kOutput, calls=%fused_computation.1 | convolution fusion | flops 9664724992 | bytes 12058624 | tf_op jit(solution)/shard_map/frn,ncm->frcm/dot_general | solution.py:24
  69.8 0.0 reduce-scatter.2.cloned.1.call-update
  69.9 0.6 fusion.21.e_ref
  70.5 40.1 %reduce-scatter.2.cloned.1.call-done = f32[16,48,2,128]{3,1,2,0:T(8,128)} async-done(((f32[16,48,2,1024]{3,1,2,0:T(8,128)}), f32[16,48,2,128]{3,1,2,0:T(8,128)}) %reduce-scatter.2.cloned.1.call-update) | async-done | bytes 786448 | tf_op jit(solution)/shard_map/reduce_scatter | solution.py:244
  110.6 1.2 convert_element_type.32
  111.8 0.5 copy.19
  112.3 1.2 copy.20
  113.5 67.1 %shard_map.46 = f32[8,256,128]{2,1,0:T(8,128)} custom-call(bf16[8,32,16,48]{3,2,1,0:T(8,128)(2,1)} %bitcast.28, bf16[48,768]{1,0:T(8,128)(2,1)} %fusion.21.e_ref, bf16[48,128,1024]{2,1,0:T(8,128)(2,1)} %leg_hbm.1), custom_call_target="tpu_custom_call" | custom-call | tf_op jit(solution)/shard_map/pallas_call | solution.py:211
  180.6 2.5 %reshape.251 = f32[4,2,16,16,2,64]{5,4,3,2,1,0:T(2,128)S(1)} reshape(f32[8,256,128]{2,1,0:T(8,128)} %shard_map.46) | data formatting | bytes 2097152 | tf_op jit(solution)/shard_map/reshape | solution.py:233
  183.1 1.6 copy.21
  184.7 2.7 %copy.22 = f32[64,16,2,128]{3,2,1,0:T(2,128)} copy(f32[64,16,2,128]{0,3,2,1:T(8,128)} %bitcast.27) | data formatting | bytes 2097152 | tf_op jit(solution)/shard_map/reshape | solution.py:234
  (6 shorter events, 0.0 us)
Async XLA Ops:
  15.1 38.4 %all-to-all-start = ((f32[16,64,512]{2,0,1:T(8,128)}), f32[16,64,512]{2,0,1:T(8,128)S(1)}, u32[]{:S(2)}, u32[]{:S(2)}) async-start(f32[16,64,512]{2,0,1:T(8,128)} %copy.17), calls=%async_computation | async-start | bytes 4194304 | tf_op jit(solution)/shard_map/all_to_all | solution.py:43
  23.1 87.5 %reduce-scatter.2.cloned.1.call-start = ((), (), s32[]{:S(2)}) async-start(), calls=%async_computation.2 | async-start | bytes 7077888 | tf_op jit(solution)/shard_map/reduce_scatter | solution.py:244
  53.5 3.0 %copy-start = (f32[512,1,1024]{2,0,1:T(8,128)S(1)}, f32[512,1,1024]{2,0,1:T(8,128)}, u32[]{:S(2)}) copy-start(f32[512,1,1024]{2,0,1:T(8,128)} %get-tuple-element.9) | copy-start | bytes 6291460
Sparse Core Ops, SparseCore 0:
  70.0 40.5 reduce-scatter.1

commit v2 on v1

--- a/solution.py
+++ b/solution.py
@@ -2,76 +2,317 @@
 
 import jax
 import jax.numpy as jnp
+import numpy as np
 from jax import lax
 from jax.experimental import pallas as pl
 from jax.experimental.pallas import tpu as pltpu
 from jax.sharding import PartitionSpec as P
 
 NLON = 4096
-M = 1024
-
-
-def twiddle(first, count):
-    longitudes = first + jnp.arange(count, dtype=jnp.int32)
-    orders = jnp.arange(M, dtype=jnp.int32)
-    product = longitudes[:, None] * orders[None, :] % NLON
-    angle = product.astype(jnp.float32) * (2.0 * math.pi / NLON)
-    scale = 1.0 / math.sqrt(NLON)
-    return jnp.stack([jnp.cos(angle) * scale, -jnp.sin(angle) * scale], axis=1)
-
-
-def transform(values, table):
-    return jnp.einsum("frn,ncm->frcm", values, table, precision=lax.Precision.HIGHEST)
-
-
-def pack_cycles(masked, plan, slot_dev):
-    n_blk = lax.axis_size("blk")
-    own_index = lax.axis_index("blk")
-    cycle_dev = masked.shape[1]
-    cap = (cycle_dev + n_blk - 1) // n_blk
-    grid = plan.reshape(n_blk, cycle_dev)
-    owner = grid // slot_dev
-    positions = jnp.arange(cycle_dev, dtype=jnp.int32)
-    earlier = positions[None, :] < positions[:, None]
-    same_owner = owner[:, :, None] == owner[:, None, :]
-    rank = jnp.sum(same_owner & earlier[None], axis=2, dtype=jnp.int32)
-    send_pos = owner * cap + rank
-    local_pos = lax.dynamic_index_in_dim(send_pos, own_index, 0, keepdims=False)
-    buffer_ids = jnp.arange(n_blk * cap, dtype=jnp.int32)
-    send_onehot = (buffer_ids[:, None] == local_pos[None, :]).astype(jnp.float32)
-    outgoing = jnp.einsum("qr,frn->fqn", send_onehot, masked, precision=lax.Precision.HIGHEST)
-    arrived = lax.all_to_all(outgoing, "blk", split_axis=1, concat_axis=1, tiled=True)
-    source_pos = (jnp.arange(n_blk, dtype=jnp.int32)[:, None] * cap + rank).reshape(-1)
-    mine = (owner == own_index).reshape(-1)
-    slot_local = (grid % slot_dev).reshape(-1)
-    slot_ids = jnp.arange(slot_dev, dtype=jnp.int32)
-    slot_onehot = ((slot_local[None, :] == slot_ids[:, None]) & mine[None, :]).astype(jnp.float32)
-    source_onehot = (source_pos[:, None] == buffer_ids[None, :]).astype(jnp.float32)
-    receive_map = jnp.dot(slot_onehot, source_onehot, precision=lax.Precision.HIGHEST)
-    return jnp.einsum("pq,fqn->fpn", receive_map, arrived, precision=lax.Precision.HIGHEST)
-
-
 MESH = pl.DeviceIdType.MESH
 BF = jnp.bfloat16
 F32 = jnp.float32
 NBLOCK = 8
 
 
-def contract_kernel(spec_ref, e_ref, leg_hbm, out_ref, leg, q, q2, ms1, mr1, ss1, sr1, ms2, mr2, ss2, sr2,
-                    leg_sem, s_sem, r_sem):
+def dft_tables():
+    r = np.arange(16)[:, None, None]
+    column = np.arange(128)[None, :, None]
+    owner, w, c, ql = column // 16, column // 8 % 2, column // 4 % 2, column % 4
+    residue = np.where(w == 0, r, np.where(r == 0, 16, 32 - r))
+    m = 32 * (4 * owner + ql) + residue
+    i = np.arange(128)[None, None, :]
+    angle = 2.0 * np.pi * (m * i % NLON) / NLON
+    cos, sin = np.cos(angle) / 64.0, np.sin(angle) / 64.0
+    real = np.where(c == 0, cos, -sin)
+    imag = np.where(c == 0, sin, cos)
+    imag = np.where(w == 0, imag, -imag)
+    real, imag = (
+        np.where((r == 0) & (w == 1), 0.0, real),
+        np.where(r == 0, np.where(w == 1, np.where(c == 0, cos, -sin), 0.0), imag),
+    )
+    table = np.concatenate([real, imag], axis=2).astype(np.float32)
+    high = table.astype(jnp.bfloat16)
+    low = (table - high.astype(np.float32)).astype(jnp.bfloat16)
+    return high, low
+
+
+def order_permutation():
+    out = np.zeros((256, 256), np.float32)
+    for r in range(16):
+        for w in range(2):
+            for c in range(2):
+                for ql in range(4):
+                    m = r if w == 0 else (16 - r) % 16
+                    out[(2 * ql + w) * 32 + c * 16 + m, r * 16 + w * 8 + c * 4 + ql] = 1.0
+    return out.astype(jnp.bfloat16)
+
+
+def real_dft(values):
+    n = len(values)
+    if n == 2:
+        return [(values[0] + values[1], None), (values[0] - values[1], None)]
+    even, odd = real_dft(values[0::2]), real_dft(values[1::2])
+    half = n // 2
+
+    def term(part, k):
+        if k <= half // 2:
+            return part[k]
+        re, im = part[half - k]
+        return re, (None if im is None else -im)
+
+    result = [None] * (half + 1)
+    for k in range(half // 2 + 1):
+        er, ei = even[k]
+        qr, qi = odd[k]
+        cos, sin = math.cos(2 * math.pi * k / n), math.sin(2 * math.pi * k / n)
+        if k == 0:
+            result[0] = (er + qr, None)
+            result[half] = (er - qr, None)
+            continue
+        if 4 * k == n:
+            tr, ti = qi, -qr
+        else:
+            tr = qr * cos + qi * sin if qi is not None else qr * cos
+            ti = qi * cos - qr * sin if qi is not None else -(qr * sin)
+
+        def add(a, b, sign):
+            if a is None:
+                return None if b is None else (b if sign > 0 else -b)
+            if b is None:
+                return a
+            return a + b if sign > 0 else a - b
+
+        result[k] = (add(er, tr, 1), add(ei, ti, 1))
+        if k != half - k:
+            ni = add(ei, ti, -1)
+            result[half - k] = (add(er, tr, -1), None if ni is None else -ni)
+    return result
+
+
+def spectrum_kernel(field_ref, mask_ref, high_ref, low_ref, perm_ref, place_ref, out_ref,
+                    masked, xr, relay, ycat, terms, sbuf, srecv,
+                    far_s, far_r, near_s, near_r, fwd_s, fwd_r, side_s, side_r, ex_s, ex_r):
+    me = lax.axis_index("order")
+    y = me // 2
+    core = me % 2
+    barrier = pltpu.get_barrier_semaphore()
+    peers = [(dy, dc) for dy in range(4) for dc in range(2) if (dy, dc) != (0, 0)]
+
+    def at(dy, other):
+        return {"order": (y + dy) % 4 * 2 + other}
+
+    for dy, dc in peers:
+        pl.semaphore_signal(barrier, inc=1, device_id=at(dy, (core + dc) % 2), device_id_type=MESH)
+
+    ocean = mask_ref[...].astype(F32)
+
+    def mask_field(f, carry):
+        masked[f] = field_ref[f] * ocean
+        return carry
+
+    lax.fori_loop(0, 16, mask_field, 0)
+    pl.semaphore_wait(barrier, 7)
+
+    halves = (pl.ds(0, 32), pl.ds(32, 32))
+    steps = (1, 3)
+
+    def remote(src, dst, ss, rs, device):
+        return pltpu.make_async_remote_copy(src_ref=src, dst_ref=dst, send_sem=ss, recv_sem=rs,
+                                            device_id=device, device_id_type=MESH)
+
+    def far(g, d, other):
+        target = ((y + 2) % 4 * 2 + other) * 2 + g
+        return remote(masked.at[target, halves[d]], relay.at[g, d, core], far_s.at[g, d, other], far_r.at[g, d, core],
+                      at(steps[d], other))
+
+    def near(g, d, other):
+        target = ((y + steps[d]) % 4 * 2 + other) * 2 + g
+        return remote(masked.at[target], xr.at[g, me], near_s.at[g, d, other], near_r.at[g, d, core],
+                      at(steps[d], other))
+
+    def forward(g, d, source):
+        origin = (y + 4 - steps[d]) % 4 * 2 + source
+        return remote(relay.at[g, d, source], xr.at[g, origin, halves[d]], fwd_s.at[g, d, source], fwd_r.at[g, d, source],
+                      at(steps[d], core))
+
+    def side(g):
+        target = (y * 2 + 1 - core) * 2 + g
+        return remote(masked.at[target], xr.at[g, me], side_s.at[g], side_r.at[g], at(0, 1 - core))
+
+    def wait_far(g, d, source):
+        remote(masked.at[0, halves[d]], relay.at[g, d, source], far_s.at[g, d, source], far_r.at[g, d, source],
+               at(steps[d], source)).wait_recv()
+
+    def wait_near(g, d, source):
+        remote(masked.at[0], xr.at[g, me], near_s.at[g, d, source], near_r.at[g, d, source],
+               at(steps[d], source)).wait_recv()
+
+    for g in range(2):
+        for d in range(2):
+            for other in range(2):
+                far(g, d, other).start()
+        for d in range(2):
+            for other in range(2):
+                near(g, d, other).start()
+        side(g).start()
+    for g in range(2):
+        xr[g, me] = masked[me * 2 + g]
+
+    for g in range(2):
+        for d in range(2):
+            for source in range(2):
+                wait_far(g, d, source)
+                forward(g, d, source).start()
+    for g in range(2):
+        for d in range(2):
+            for source in range(2):
+                wait_near(g, d, source)
+        side(g).wait_recv()
+        for d in range(2):
+            for source in range(2):
+                forward(g, d, source).wait_recv()
+
+        def butterfly(k, carry):
+            rows = pl.ds(pl.multiple_of(16 * k, 16), 16)
+            values = [xr[g, a // 4, rows, 128 * (a % 4):128 * (a % 4) + 128] for a in range(32)]
+            result = real_dft(values)
+            out_rows = pl.ds(pl.multiple_of(64 * g + 16 * k, 16), 16)
+            for r in range(16):
+                pair = (result[0][0], result[16][0]) if r == 0 else result[r]
+                for part, value in enumerate(pair):
+                    high = value.astype(BF)
+                    ycat[r, out_rows, 128 * part:128 * part + 128] = high
+                    ycat[r, out_rows, 256 + 128 * part:384 + 128 * part] = (value - high.astype(F32)).astype(BF)
+            return carry
+
+        lax.fori_loop(0, 4, butterfly, 0)
+
+    contract_lanes = (((1,), (1,)), ((), ()))
+
+    def transform(r, carry):
+        yh, yl = ycat[r, :, 0:256], ycat[r, :, 256:512]
+        th, tl = high_ref[r], low_ref[r]
+        out = lax.dot_general(th, yh, contract_lanes, preferred_element_type=F32)
+        out += lax.dot_general(th, yl, contract_lanes, preferred_element_type=F32)
+        out += lax.dot_general(tl, yh, contract_lanes, preferred_element_type=F32)
+        terms[:, r] = out.astype(BF).reshape(8, 16, 128)
+        return carry
+
+    lax.fori_loop(0, 16, transform, 0)
+
+    def arrange(o, carry):
+        part = jnp.dot(perm_ref[...], terms[o].reshape(256, 128), preferred_element_type=F32)
+        sbuf[o] = part.astype(BF).reshape(8, 32, 128)
+        return carry
+
+    lax.fori_loop(0, 8, arrange, 0)
+
+    def exchange(dy, dc):
+        target = (y + dy) % 4 * 2 + (core + dc) % 2
+        return remote(sbuf.at[target], srecv.at[me], ex_s.at[dy, dc], ex_r.at[dy, dc], {"order": target})
+
+    for dy, dc in peers:
+        exchange(dy, dc).start()
+    srecv[me] = sbuf[me]
+    for dy, dc in peers:
+        exchange(dy, dc).wait_recv()
+
+    def place(tt, carry):
+        parts = []
+        for h in range(2):
+            rows = srecv[:, tt + 4 * h].reshape(256, 128)
+            out = lax.dot_general(place_ref[...], rows, contract_lanes, preferred_element_type=F32)
+            parts.append(out.reshape(16, 8, 256))
+        out_ref[:, tt] = jnp.concatenate(parts, axis=1).astype(BF)
+        return carry
+
+    lax.fori_loop(0, 4, place, 0)
+
+    for g in range(2):
+        for d in range(2):
+            for other in range(2):
+                far(g, d, other).wait_send()
+                near(g, d, other).wait_send()
+                forward(g, d, other).wait_send()
+        side(g).wait_send()
+    for dy, dc in peers:
+        exchange(dy, dc).wait_send()
+
+
+def spectrum_blocks(field, mask, place):
+    high, low = dft_tables()
+    vmem = pl.BlockSpec(memory_space=pltpu.VMEM)
+    dma = pltpu.SemaphoreType.DMA
+    return pl.pallas_call(
+        spectrum_kernel,
+        out_shape=jax.ShapeDtypeStruct((16, 4, 16, 256), BF),
+        in_specs=[vmem] * 6,
+        out_specs=vmem,
+        scratch_shapes=[
+            pltpu.VMEM((16, 64, 512), F32),
+            pltpu.VMEM((2, 8, 64, 512), F32),
+            pltpu.VMEM((2, 2, 2, 32, 512), F32),
+            pltpu.VMEM((16, 128, 512), BF),
+            pltpu.VMEM((8, 16, 16, 128), BF),
+            pltpu.VMEM((8, 8, 32, 128), BF),
+            pltpu.VMEM((8, 8, 32, 128), BF),
+            dma((2, 2, 2)), dma((2, 2, 2)), dma((2, 2, 2)), dma((2, 2, 2)), dma((2, 2, 2)), dma((2, 2, 2)),
+            dma((2,)), dma((2,)), dma((4, 2)), dma((4, 2)),
+        ],
+        compiler_params=pltpu.CompilerParams(collective_id=1, has_side_effects=True, vmem_limit_bytes=40 * 2**20),
+    )(field, mask, jnp.asarray(high), jnp.asarray(low), jnp.asarray(order_permutation()), place)
+
+
+def plan_maps(plan):
+    own = lax.axis_index("blk")
+    grid = plan.reshape(16, 64)
+    owner = grid // 48
+    positions = jnp.arange(64, dtype=jnp.int32)
+    earlier = positions[None, :] < positions[:, None]
+    rank = jnp.sum((owner[:, :, None] == owner[:, None, :]) & earlier[None], axis=2, dtype=jnp.int32)
+    own_owner = lax.dynamic_index_in_dim(owner, own, 0, keepdims=False)
+    own_rank = lax.dynamic_index_in_dim(rank, own, 0, keepdims=False)
+    row = jnp.arange(128, dtype=jnp.int32)[:, None]
+    match = (own_owner[None, :] == row // 8) & (own_rank[None, :] == row // 2 % 4)
+    place = jnp.concatenate([match & (row % 2 == 0), match & (row % 2 == 1)], axis=1).astype(BF)
+    ranks = jnp.arange(4, dtype=jnp.int32)
+    to_rank = ((rank[:, None, :] == ranks[None, :, None]) & (owner == own)[:, None, :]).astype(BF)
+    to_slot = ((grid % 48)[:, :, None] == jnp.arange(768, dtype=jnp.int32)[None, None, :] // 16).astype(BF)
+    expand = jnp.einsum("brc,bcp->brp", to_rank, to_slot, preferred_element_type=F32).astype(BF)
+    expand = jnp.broadcast_to(expand[:, None, :, None, :], (16, 2, 4, 2, 768)).reshape(256, 768)
+    return place, expand
+
+
+def contract_kernel(sent_ref, e_ref, leg_hbm, out_ref, arrived, leg, q, q2, ms1, mr1, ss1, sr1, ms2, mr2, ss2, sr2,
+                    leg_sem, ex_s, ex_r, s_sem, r_sem):
     me = lax.axis_index("blk")
     x = me // 4
     z = me % 4
     for t in range(8):
         pltpu.make_async_copy(leg_hbm.at[:, pl.ds(16 * t, 16), :], leg.at[t], leg_sem.at[t]).start()
     barrier = pltpu.get_barrier_semaphore()
-    for nx, nz in ((1, 0), (3, 0), (0, 1), (0, 3)):
-        pl.semaphore_signal(barrier, inc=1, device_id={"blk": (x + nx) % 4 * 4 + (z + nz) % 4}, device_id_type=MESH)
-    pl.semaphore_wait(barrier, 4)
+    peers = [(dx, dz) for dx in range(4) for dz in range(4) if (dx, dz) != (0, 0)]
+    for dx, dz in peers:
+        pl.semaphore_signal(barrier, inc=1, device_id={"blk": (x + dx) % 4 * 4 + (z + dz) % 4}, device_id_type=MESH)
+    pl.semaphore_wait(barrier, 15)
+
+    def exchange(dx, dz):
+        target = (x + dx) % 4 * 4 + (z + dz) % 4
+        return pltpu.make_async_remote_copy(
+            src_ref=sent_ref.at[target], dst_ref=arrived.at[me], send_sem=ex_s.at[dx, dz], recv_sem=ex_r.at[dx, dz],
+            device_id={"blk": target}, device_id_type=MESH)
+
+    for dx, dz in peers:
+        exchange(dx, dz).start()
+    arrived[me] = sent_ref[me]
+    for dx, dz in peers:
+        exchange(dx, dz).wait_recv()
 
     rows = lax.broadcasted_iota(jnp.int32, (256, 768), 0) % 16
     lanes = lax.broadcasted_iota(jnp.int32, (256, 768), 1) % 16
     mask = rows == lanes
+    place = lax.broadcasted_iota(jnp.int32, (256, 768), 0)
     low = lax.broadcasted_iota(jnp.int32, (256, 128), 1) < 64
 
     def neighbour(axis, step):
@@ -102,10 +343,10 @@
                 pltpu.make_async_copy(leg_hbm.at[:, pl.ds(16 * t, 16), :], leg.at[t], leg_sem.at[t]).wait()
 
         lhs = []
+        values = arrived[:, tt].reshape(256, 256)
         for h in (0, 1):
-            sp = spec_ref[tt + 4 * h, pl.ds(16 * par, 16)]
-            sp = sp.reshape(256, sp.shape[-1])
-            ex = jnp.dot(sp, e_ref[...], preferred_element_type=F32)
+            expand = jnp.where((place // 8 % 2 == h) & (place % 2 == par), e_ref[...].astype(F32), 0.0).astype(BF)
+            ex = lax.dot_general(values, expand, (((0,), (0,)), ((), ())), preferred_element_type=F32)
             lhs.append(jnp.where(mask, ex, 0.0).astype(BF))
         for bx in range(4):
             pa, pb = [
@@ -202,9 +443,11 @@
         return carry
 
     lax.fori_loop(0, NBLOCK, drain, 0)
-
-
-def contract(spec, expand, legendre):
+    for dx, dz in peers:
+        exchange(dx, dz).wait_send()
+
+
+def contract(sent, expand, legendre):
     big = (NBLOCK, 2, 2, 4, 128, 128)
     small = (NBLOCK, 2, 2, 128, 128)
     vmem = pl.BlockSpec(memory_space=pltpu.VMEM)
@@ -214,6 +457,7 @@
         in_specs=[vmem, vmem, pl.BlockSpec(memory_space=pl.ANY)],
         out_specs=vmem,
         scratch_shapes=[
+            pltpu.VMEM((16, 4, 16, 256), BF),
             pltpu.VMEM((8, 48, 16, 1024), BF),
             pltpu.VMEM((4, 4, 4, 256, 128), F32),
             pltpu.VMEM((NBLOCK, 4, 256, 128), F32),
@@ -222,32 +466,24 @@
             pltpu.VMEM(small, BF), pltpu.VMEM(small, BF),
             pltpu.VMEM((NBLOCK, 2, 128, 128), BF), pltpu.VMEM((NBLOCK, 2, 128, 128), BF),
             pltpu.SemaphoreType.DMA((8,)),
+            pltpu.SemaphoreType.DMA((4, 4)),
+            pltpu.SemaphoreType.DMA((4, 4)),
             pltpu.SemaphoreType.DMA((NBLOCK, 4, 2)),
             pltpu.SemaphoreType.DMA((NBLOCK, 4, 2)),
         ],
         compiler_params=pltpu.CompilerParams(collective_id=0, has_side_effects=True, vmem_limit_bytes=60 * 2**20),
-    )(spec, expand, legendre)
+    )(sent, expand, legendre)
 
 
 def finish(blocks):
-    blocks = blocks.reshape(4, 2, 16, 16, 2, 64)
-    return jnp.transpose(blocks, (5, 1, 2, 4, 0, 3)).reshape(64, 16, 2, 128)
+    blocks = blocks.reshape(4, 2, 8, 2, 16, 2, 64)
+    return jnp.transpose(blocks, (6, 2, 1, 3, 5, 0, 4)).reshape(64, 16, 2, 128)
 
 
 def body(field, ocean_mask, plan, legendre):
-    lon_local = field.shape[2]
-    slot_dev = legendre.shape[0]
-    masked = field * ocean_mask.astype(jnp.float32)[None]
-    packed = pack_cycles(masked, plan, slot_dev)
-    first = lax.axis_index("order") * lon_local
-    terms = transform(packed, twiddle(first, lon_local))
-    spectrum = lax.psum_scatter(terms, "order", scatter_dimension=3, tiled=True).astype(
-        jnp.bfloat16
-    )
-    spec = spectrum.reshape(16, 48, 2, 8, 16).transpose(3, 0, 2, 4, 1).reshape(8, 32, 16, 48)
-    slots = jnp.arange(48, dtype=jnp.int32)[:, None]
-    expand = (slots == jnp.arange(768, dtype=jnp.int32)[None, :] // 16).astype(BF)
-    return finish(contract(spec, expand, legendre))
+    place, expand = plan_maps(plan)
+    sent = spectrum_blocks(field, ocean_mask, place)
+    return finish(contract(sent, expand, legendre))
 
 
 def solution(mesh):

time: 195 us -> 138 us (0.71)
  waiting for transfers between devices: 59 us -> 0 us
  Pallas kernels: 67.1 us -> 121 us
  matrix products: 19.6 us -> 0.66 us
  between operations: 13.5 us -> 0.09 us
  other arithmetic: 15.5 us -> 2.32 us
  starting transfers between devices: 8.21 us -> 0 us
    pallas_call x0 -> x1, Pallas kernels: none -> 41.6 us  [spectrum_blocks(): pl.pallas_call(spectrum_kernel, out_shape=jax.ShapeDtypeStruct((16, 4, 16...]
    reduce_scatter x1 -> x0, waiting for transfers between devices: 40.1 us -> none  [body(): lax.psum_scatter(terms, 'order', scatter_dimension=3, tiled=True)]
    dot_general x4 -> x1, matrix products: 19.6 us -> 0.66 us  [plan_maps(): jnp.einsum('brc,bcp->brp', to_rank, to_slot, preferred_element_type=F32)]
    all_to_all x1 -> x0, waiting for transfers between devices: 18.9 us -> none  [pack_cycles(): lax.all_to_all(outgoing, 'blk', split_axis=1, concat_axis=1, tiled=True)]
    pallas_call x1, Pallas kernels: 67.1 us -> 79.5 us  [contract(): pl.pallas_call(contract_kernel, out_shape=jax.ShapeDtypeStruct((NBLOCK, 2...]
    mul x2 -> x0, other arithmetic: 10.8 us -> none  [the longest x1 10.8 us: twiddle(): return jnp.stack([jnp.cos(angle) * scale, -jnp.sin(angle) * scale], axis=1)]
    all_to_all x1 -> x0, starting transfers between devices: 7.99 us -> none  [pack_cycles(): lax.all_to_all(outgoing, 'blk', split_axis=1, concat_axis=1, tiled=True)]
    unnamed x2 -> x12, local copies, waits for them, and re-layouts: 0.01 us -> 5.05 us
  transfers between devices with their start and end apart: 2 -> 0, of which waited for: 2 -> 0; matrix products, arithmetic and copies ran while one was open for 6% -> 0% of each run, Pallas kernels for 0% -> 0%
where the time goes in v2:
time: 138 us; the launch traced here: 137 us
  Pallas kernels  121 us (88%)
  local copies, waits for them, and re-layouts  13.2 us (10%)
  other arithmetic  2.32 us (2%)
    pallas_call x1, Pallas kernels, contract(): pl.pallas_call(contract_kernel, out_shape=jax.ShapeDtypeStruct((NBLOCK, 2...  79.5 us
    pallas_call x1, Pallas kernels, spectrum_blocks(): pl.pallas_call(spectrum_kernel, out_shape=jax.ShapeDtypeStruct((16, 4, 16...  41.6 us
    unnamed x12, local copies, waits for them, and re-layouts  5.05 us
    reshape x2, local copies, waits for them, and re-layouts, finish(): blocks = blocks.reshape(4, 2, 8, 2, 16, 2, 64)  4.12 us

profile of v2, /device:TPU:0, one launch (start us, length us, event | category | flops | bytes accessed | tf_op | source)
XLA Modules:
  0.0 137.4 jit_solution(4094040257411821088)
XLA Ops:
  0.0 0.0 copy-start.1
  0.0 0.8 sign_compare_fusion
  0.8 0.1 ne.169
  1.0 0.7 broadcast_remainder_fusion
  1.7 0.1 rem.86
  1.7 0.1 div.41
  1.8 0.5 convert_reduce_fusion
  2.4 0.1 fusion.8
  2.5 0.1 add_convert_fusion.place_ref
  2.6 0.7 fusion.4
  3.3 0.2 broadcast_in_dim.2
  3.5 0.9 reshape.225.e_ref
  4.4 0.0 copy-done.1
  4.4 0.0 copy-start.2
  4.4 1.2 copy-done.2
  5.6 0.0 copy-start.3
  5.6 1.2 copy-done.3
  6.8 0.0 copy-start.4
  6.8 0.9 copy-done.4
  7.7 0.0 copy-start.5
  7.7 0.9 copy-done.5
  8.7 41.6 %shard_map.73.sent_ref = bf16[16,4,16,256]{3,2,1,0:T(8,128)(2,1)S(1)} custom-call(f32[16,64,512]{2,1,0:T(8,128)S(1)} %copy-done.1, s32[64,512]{1,0:T(8,128)S(1)} %copy-done.4, bf16[16,128,256]{2,1,0:T(8,128)(2,1)S(1)} %copy-done.3, bf16[16,128,256]{2,1,0:T(8,128)(2,1)S(1)} %copy-done.2, bf16[256,256]{1,0:T(8,128)(2,1)S(1)} %copy-done.5, ...), custom_call_target="tpu_custom_call" | custom-call | tf_op jit(solution)/shard_map/pallas_call | solution.py:247
  50.3 0.0 copy-start
  50.3 0.8 copy-done
  51.1 79.5 %shard_map.74 = f32[8,256,128]{2,1,0:T(8,128)} custom-call(bf16[16,4,16,256]{3,2,1,0:T(8,128)(2,1)} %copy-done, bf16[256,768]{1,0:T(8,128)(2,1)} %reshape.225.e_ref, bf16[48,128,1024]{2,1,0:T(8,128)(2,1)} %leg_hbm.1), custom_call_target="tpu_custom_call" | custom-call | tf_op jit(solution)/shard_map/pallas_call | solution.py:454
  130.5 2.5 %reshape.226 = f32[4,2,8,2,16,2,64]{6,5,4,3,2,1,0:T(2,128)S(1)} reshape(f32[8,256,128]{2,1,0:T(8,128)} %shard_map.74) | data formatting | bytes 2097152 | tf_op jit(solution)/shard_map/reshape | solution.py:479
  133.1 1.6 %copy.14 = f32[4,2,8,2,16,2,64]{6,4,0,5,3,1,2:T(8,128)} copy(f32[4,2,8,2,16,2,64]{6,5,4,3,2,1,0:T(2,128)S(1)} %reshape.226) | data formatting | bytes 2097152 | tf_op jit(solution)/shard_map/reshape | solution.py:479
  134.7 2.7 %copy.15 = f32[64,16,2,128]{3,2,1,0:T(2,128)} copy(f32[64,16,2,128]{0,3,2,1:T(8,128)} %bitcast.7) | data formatting | bytes 2097152 | tf_op jit(solution)/shard_map/reshape | solution.py:480
  (7 shorter events, 0.1 us)
Async XLA Ops:
  0.0 4.4 %copy-start.1 = (f32[16,64,512]{2,1,0:T(8,128)S(1)}, f32[16,64,512]{2,1,0:T(8,128)}, u32[]{:S(2)}) copy-start(f32[16,64,512]{2,1,0:T(8,128)} %field_ref.1) | copy-start | bytes 6291460
  4.4 1.2 copy-start.2
  5.6 1.2 copy-start.3
  6.8 0.9 copy-start.4
  7.7 0.9 copy-start.5
  50.3 0.8 copy-start

commit v3 on v1

v3 whole, which is shorter than its diff:
```python
import math

import jax
import jax.numpy as jnp
import numpy as np
from jax import lax
from jax.experimental import pallas as pl
from jax.experimental.pallas import tpu as pltpu
from jax.sharding import PartitionSpec as P

NLON = 4096
MESH = pl.DeviceIdType.MESH
BF = jnp.bfloat16
F32 = jnp.float32
NBLOCK = 8
CONTRACT_LANES = (((1,), (1,)), ((), ()))
CONTRACT_ROWS = (((0,), (0,)), ((), ()))

STEP_A, STEP_B, STEP_C, DELAY = 7, 8, 11, 4
LAGS = (0, 4, 6, 8, 10)
FIRST = 3


def dft_tables():
    r = np.arange(16)[:, None, None]
    column = np.arange(128)[None, :, None]
    owner, w, c, ql = column // 16, column // 8 % 2, column // 4 % 2, column % 4
    residue = np.where(w == 0, r, np.where(r == 0, 16, 32 - r))
    m = 32 * (4 * owner + ql) + residue
    i = np.arange(128)[None, None, :]
    angle = 2.0 * np.pi * (m * i % NLON) / NLON
    cos, sin = np.cos(angle) / 64.0, np.sin(angle) / 64.0
    real = np.where(c == 0, cos, -sin)
    imag = np.where(c == 0, sin, cos)
    imag = np.where(w == 0, imag, -imag)
    real, imag = (
        np.where((r == 0) & (w == 1), 0.0, real),
        np.where(r == 0, np.where(w == 1, np.where(c == 0, cos, -sin), 0.0), imag),
    )
    table = np.concatenate([real, imag], axis=2).astype(np.float32)
    high = table.astype(jnp.bfloat16)
    low = (table - high.astype(np.float32)).astype(jnp.bfloat16)
    return high, low


def order_permutation():
    out = np.zeros((128, 128), np.float32)
    for r in range(8):
        for w in range(2):
            for c in range(2):
                for ql in range(4):
                    mh = r if w == 0 else (8 - r) % 8
                    out[(2 * ql + w) * 16 + c * 8 + mh, r * 16 + w * 8 + c * 4 + ql] = 1.0
    return out.astype(jnp.bfloat16)


def real_dft(values):
    n = len(values)
    if n == 2:
        return [(values[0] + values[1], None), (values[0] - values[1], None)]
    even, odd = real_dft(values[0::2]), real_dft(values[1::2])
    half = n // 2

    def term(part, k):
        if k <= half // 2:
            return part[k]
        re, im = part[half - k]
        return re, (None if im is None else -im)

    result = [None] * (half + 1)
    for k in range(half // 2 + 1):
        er, ei = even[k]
        qr, qi = odd[k]
        cos, sin = math.cos(2 * math.pi * k / n), math.sin(2 * math.pi * k / n)
        if k == 0:
            result[0] = (er + qr, None)
            result[half] = (er - qr, None)
            continue
        if 4 * k == n:
            tr, ti = qi, -qr
        else:
            tr = qr * cos + qi * sin if qi is not None else qr * cos
            ti = qi * cos - qr * sin if qi is not None else -(qr * sin)

        def add(a, b, sign):
            if a is None:
                return None if b is None else (b if sign > 0 else -b)
            if b is None:
                return a
            return a + b if sign > 0 else a - b

        result[k] = (add(er, tr, 1), add(ei, ti, 1))
        if k != half - k:
            ni = add(ei, ti, -1)
            result[half - k] = (add(er, tr, -1), None if ni is None else -ni)
    return result


def kernel(field_hbm, mask_hbm, plan_ref, high_hbm, low_hbm, perm_hbm, leg_hbm, out_ref,
           masked, mask, high, low, perm, xr, relay, ycat, terms, sbuf, srecv, place, expand, sent, arrived,
           leg, q, q2, ms1, mr1, ss1, sr1, ms2, mr2, ss2, sr2, final,
           field_sem, load_sem, leg_sem, far_s, far_r, near_s, near_r, fwd_s, fwd_r, side_s, side_r,
           ox_s, ox_r, bx_s, bx_r, ring_s, ring_r):
    order = lax.axis_index("order")
    y, core = order // 2, order % 2
    me = lax.axis_index("blk")
    x, z = me // 4, me % 4

    def load_field(g, o):
        f = 2 * o + g
        return pltpu.make_async_copy(field_hbm.at[f], masked.at[f], field_sem.at[f])

    loads = [pltpu.make_async_copy(src, dst, load_sem.at[i]) for i, (src, dst) in enumerate(
        ((mask_hbm, mask), (high_hbm, high), (low_hbm, low), (perm_hbm, perm)))]

    def load_leg(t):
        return pltpu.make_async_copy(leg_hbm.at[:, pl.ds(16 * t, 16), :], leg.at[t], leg_sem.at[t])

    loads[0].start()
    for g in range(2):
        for o in range(8):
            load_field(g, o).start()
    for copy in loads[1:]:
        copy.start()
    for t in range(8):
        load_leg(t).start()

    barrier = pltpu.get_barrier_semaphore()
    order_peers = [(dy, dc) for dy in range(4) for dc in range(2) if (dy, dc) != (0, 0)]
    blk_peers = [(dx, dz) for dx in range(4) for dz in range(4) if (dx, dz) != (0, 0)]

    def at(dy, other):
        return {"order": (y + dy) % 4 * 2 + other}

    for dy, dc in order_peers:
        pl.semaphore_signal(barrier, inc=1, device_id=at(dy, (core + dc) % 2), device_id_type=MESH)
    for dx, dz in blk_peers:
        pl.semaphore_signal(barrier, inc=1, device_id={"blk": (x + dx) % 4 * 4 + (z + dz) % 4}, device_id_type=MESH)

    loads[0].wait()

    def mask_fields(g):
        for o in range(8):
            load_field(g, o).wait()

        def one(o, carry):
            masked[2 * o + g] = masked[2 * o + g] * mask[...].astype(F32)
            return carry

        lax.fori_loop(0, 8, one, 0)
        xr[g, order] = masked[order * 2 + g]

    def remote(src, dst, ss, rs, device):
        return pltpu.make_async_remote_copy(src_ref=src, dst_ref=dst, send_sem=ss, recv_sem=rs,
                                            device_id=device, device_id_type=MESH)

    halves = (pl.ds(0, 32), pl.ds(32, 32))
    steps = (1, 3)
    pairs = [(d, other) for d in range(2) for other in range(2)]

    def far(g, d, other):
        target = ((y + 2) % 4 * 2 + other) * 2 + g
        return remote(masked.at[target, halves[d]], relay.at[g, d, core], far_s.at[g, d, other], far_r.at[g, d, core],
                      at(steps[d], other))

    def near(g, d, other):
        target = ((y + steps[d]) % 4 * 2 + other) * 2 + g
        return remote(masked.at[target], xr.at[g, order], near_s.at[g, d, other], near_r.at[g, d, core],
                      at(steps[d], other))

    def forward(g, d, source):
        origin = (y + 4 - steps[d]) % 4 * 2 + source
        return remote(relay.at[g, d, source], xr.at[g, origin, halves[d]], fwd_s.at[g, d, source], fwd_r.at[g, d, source],
                      at(steps[d], core))

    def side(g):
        target = (y * 2 + 1 - core) * 2 + g
        return remote(masked.at[target], xr.at[g, order], side_s.at[g], side_r.at[g], at(0, 1 - core))

    def wait_far(g, d, source):
        remote(masked.at[0, halves[d]], relay.at[g, d, source], far_s.at[g, d, source], far_r.at[g, d, source],
               at(steps[d], source)).wait_recv()

    def wait_near(g, d, source):
        remote(masked.at[0], xr.at[g, order], near_s.at[g, d, source], near_r.at[g, d, source],
               at(steps[d], source)).wait_recv()

    mask_fields(0)
    pl.semaphore_wait(barrier, 22)
    for d, other in pairs:
        far(0, d, other).start()
    for d, other in pairs:
        near(0, d, other).start()
    side(0).start()
    mask_fields(1)
    for d, other in pairs:
        far(1, d, other).start()
    side(1).start()

    earlier = (lax.broadcasted_iota(jnp.int32, (64, 64), 0) < lax.broadcasted_iota(jnp.int32, (64, 64), 1))
    earlier = earlier.astype(F32).astype(BF)

    def owner_of(slots, rows):
        slots = jnp.broadcast_to(slots, (rows, 64))
        owner = jnp.zeros((rows, 64), jnp.int32)
        for b in range(1, 17):
            owner += (slots >= 48 * b).astype(jnp.int32)
        return slots, owner

    row = lax.broadcasted_iota(jnp.int32, (128, 64), 0)
    _, owner = owner_of(plan_ref[pl.ds(me, 1), :], 128)
    mine = owner == row // 8
    count = jnp.dot(mine.astype(F32).astype(BF), earlier, preferred_element_type=F32)
    match = mine & (count == (row // 2 % 4).astype(F32))
    for rh in range(2):
        place[:, 64 * rh:64 * rh + 64] = (match & (row % 2 == rh)).astype(F32).astype(BF)

    def source_map(b, carry):
        slots, owner = owner_of(plan_ref[pl.ds(b, 1), :], 16)
        mine = owner == me
        count = jnp.dot(mine.astype(F32).astype(BF), earlier, preferred_element_type=F32)
        rows = lax.broadcasted_iota(jnp.int32, (16, 64), 0)
        match = mine & (count == (rows // 2 % 4).astype(F32))
        slot = jnp.sum(jnp.where(match, (slots - 48 * me + 1).astype(F32), 0.0), axis=1, keepdims=True)
        lanes = lax.broadcasted_iota(jnp.int32, (16, 768), 1) // 16 + 1
        rows = lax.broadcasted_iota(jnp.int32, (16, 768), 0)
        hit = jnp.broadcast_to(slot, (16, 768)) == lanes.astype(F32)
        for h in range(2):
            for rh in range(2):
                expand[h, rh, pl.ds(pl.multiple_of(16 * b, 16), 16), :] = (
                    hit & (rows // 8 == h) & (rows % 2 == rh)).astype(F32).astype(BF)
        return carry

    lax.fori_loop(0, 16, source_map, 0)
    for copy in loads[1:]:
        copy.wait()

    def exchange_order(g, dy, dc):
        target = (y + dy) % 4 * 2 + (core + dc) % 2
        return remote(sbuf.at[g, target], srecv.at[g, order], ox_s.at[g, dy, dc], ox_r.at[g, dy, dc], {"order": target})

    def exchange_blk(g, dx, dz):
        target = (x + dx) % 4 * 4 + (z + dz) % 4
        return remote(sent.at[g, target], arrived.at[g, me], bx_s.at[g, dx, dz], bx_r.at[g, dx, dz], {"blk": target})

    def pass_on(g):
        for d, source in pairs:
            wait_far(g, d, source)
            forward(g, d, source).start()

    def transform_group(g):
        for d, source in pairs:
            wait_near(g, d, source)
        side(g).wait_recv()
        for d, source in pairs:
            forward(g, d, source).wait_recv()

        def butterfly(k, carry):
            rows = pl.ds(pl.multiple_of(16 * k, 16), 16)
            values = [xr[g, a // 4, rows, 128 * (a % 4):128 * (a % 4) + 128] for a in range(32)]
            result = real_dft(values)
            for r in range(16):
                pair = (result[0][0], result[16][0]) if r == 0 else result[r]
                for part, value in enumerate(pair):
                    top = value.astype(BF)
                    ycat[r, rows, 128 * part:128 * part + 128] = top
                    ycat[r, rows, 256 + 128 * part:384 + 128 * part] = (value - top.astype(F32)).astype(BF)
            return carry

        lax.fori_loop(0, 4, butterfly, 0)

        def transform(r, carry):
            parts = []
            for rr in (r, r + 8):
                yh, yl = ycat[rr, :, 0:256], ycat[rr, :, 256:512]
                out = lax.dot_general(high[rr], yh, CONTRACT_LANES, preferred_element_type=F32)
                out += lax.dot_general(high[rr], yl, CONTRACT_LANES, preferred_element_type=F32)
                out += lax.dot_general(low[rr], yh, CONTRACT_LANES, preferred_element_type=F32)
                parts.append(out)
            terms[:, r] = jnp.concatenate(parts, axis=1).astype(BF).reshape(8, 16, 128)
            return carry

        lax.fori_loop(0, 8, transform, 0)

        def arrange(o, carry):
            part = jnp.dot(perm[...], terms[o].reshape(128, 128), preferred_element_type=F32)
            sbuf[g, o] = part.astype(BF).reshape(8, 16, 128)
            return carry

        lax.fori_loop(0, 8, arrange, 0)
        for dy, dc in order_peers:
            exchange_order(g, dy, dc).start()
        srecv[g, order] = sbuf[g, order]

    def place_group(g):
        for dy, dc in order_peers:
            exchange_order(g, dy, dc).wait_recv()
        for tt in range(4):
            parts = []
            for h in range(2):
                rows = srecv[g, :, tt + 4 * h].reshape(128, 128)
                out = lax.dot_general(place[...], rows, CONTRACT_LANES, preferred_element_type=F32)
                parts.append(out.reshape(16, 8, 128))
            sent[g, :, tt] = jnp.concatenate(parts, axis=1).astype(BF)
        for dx, dz in blk_peers:
            exchange_blk(g, dx, dz).start()
        arrived[g, me] = sent[g, me]

    def receive_group(g):
        for dx, dz in blk_peers:
            exchange_blk(g, dx, dz).wait_recv()

    low_lanes = lax.broadcasted_iota(jnp.int32, (256, 128), 1) < 64

    def neighbour(axis, step):
        nx = (x + step * (1 - axis)) % 4
        nz = (z + step * axis) % 4
        return {"blk": nx * 4 + nz}

    def copies(s, kind, src, dst, axis):
        return [remote(src.at[s, way], dst.at[s, way], ring_s.at[s, kind, way], ring_r.at[s, kind, way],
                       neighbour(axis, 3 - 2 * way)) for way in range(2)]

    A, B = pl.ds(0, 128), pl.ds(128, 128)

    def compute(s):
        g, tt, par, qs = s // 4, s % 4, s % 2, s % 4

        @pl.when(s < 4)
        def _():
            load_leg(tt).wait()
            load_leg(tt + 4).wait()

        rows = lax.broadcasted_iota(jnp.int32, (256, 768), 0)
        lanes = lax.broadcasted_iota(jnp.int32, (256, 768), 1) % 16
        rh, mh = rows // 128, rows % 8
        swapped = (par == 1) & (mh > 0)
        mask = lanes == jnp.where(swapped, 8 - 8 * rh, 8 * rh) + mh
        values = arrived[g, :, tt].reshape(256, 128)
        lhs = []
        for h in range(2):
            ex = jnp.concatenate([
                lax.dot_general(values, expand[h, part], CONTRACT_ROWS, preferred_element_type=F32)
                for part in range(2)], axis=0)
            lhs.append(jnp.where(mask, ex, 0.0).astype(BF))
        for bx in range(4):
            pa, pb = [
                jnp.dot(lhs[h], leg[tt + 4 * h, :, :, 256 * bx:256 * bx + 256].reshape(768, 256),
                        preferred_element_type=F32)
                for h in range(2)
            ]
            for half in range(2):
                a = pa[:, 128 * half:128 * half + 128]
                b = pb[:, 128 * half:128 * half + 128]
                first = jnp.where(low_lanes, a, pltpu.roll(b, 64, 1))
                second = jnp.where(low_lanes, pltpu.roll(a, 64, 1), b)
                for bz, value in ((2 * half, first), (2 * half + 1, second)):
                    q[qs, bx * (1 - par) + bz * par, bz * (1 - par) + bx * par] = value
        i = x * (1 - par) + z * par
        c1, c2, c3 = (i + 1) % 4, (i + 2) % 4, (i + 3) % 4
        minus, plus = copies(s, 0, ms1, mr1, par)
        ms1[s, 0, 0] = q[qs, c2, :, A, :].astype(BF)
        ms1[s, 0, 1] = q[qs, c3, :, B, :].astype(BF)
        minus.start()
        ms1[s, 1, 0] = q[qs, c2, :, B, :].astype(BF)
        ms1[s, 1, 1] = q[qs, c1, :, A, :].astype(BF)
        plus.start()

    def relay1(s):
        par, qs = s % 2, s % 4
        i = x * (1 - par) + z * par
        c1, c3 = (i + 1) % 4, (i + 3) % 4
        minus, plus = copies(s, 0, ms1, mr1, par)
        send = copies(s, 1, ss1, sr1, par)
        minus.wait_recv()
        ss1[s, 0] = (q[qs, c3, :, A, :] + mr1[s, 0, 0].astype(F32)).astype(BF)
        send[0].start()
        plus.wait_recv()
        ss1[s, 1] = (q[qs, c1, :, B, :] + mr1[s, 1, 0].astype(F32)).astype(BF)
        send[1].start()

    def owner1(s):
        par, qs = s % 2, s % 4
        i = x * (1 - par) + z * par
        minus, plus = copies(s, 1, ss1, sr1, par)
        minus.wait_recv()
        q2[s, :, A, :] = q[qs, i, :, A, :] + mr1[s, 1, 1].astype(F32) + sr1[s, 0].astype(F32)
        plus.wait_recv()
        q2[s, :, B, :] = q[qs, i, :, B, :] + mr1[s, 0, 1].astype(F32) + sr1[s, 1].astype(F32)
        j = z * (1 - par) + x * par
        d1, d2, d3 = (j + 1) % 4, (j + 2) % 4, (j + 3) % 4
        ms2[s, 0, 0] = q2[s, d2, A, :].astype(BF)
        ms2[s, 0, 1] = q2[s, d3, B, :].astype(BF)
        ms2[s, 1, 0] = q2[s, d2, B, :].astype(BF)
        ms2[s, 1, 1] = q2[s, d1, A, :].astype(BF)
        for copy in copies(s, 2, ms2, mr2, 1 - par):
            copy.start()

    def relay2(s):
        par = s % 2
        j = z * (1 - par) + x * par
        d1, d3 = (j + 1) % 4, (j + 3) % 4
        minus, plus = copies(s, 2, ms2, mr2, 1 - par)
        send = copies(s, 3, ss2, sr2, 1 - par)
        minus.wait_recv()
        ss2[s, 0] = (q2[s, d3, A, :] + mr2[s, 0, 0].astype(F32)).astype(BF)
        send[0].start()
        plus.wait_recv()
        ss2[s, 1] = (q2[s, d1, B, :] + mr2[s, 1, 0].astype(F32)).astype(BF)
        send[1].start()

    def owner2(s):
        par = s % 2
        j = z * (1 - par) + x * par
        minus, plus = copies(s, 3, ss2, sr2, 1 - par)
        minus.wait_recv()
        final[s, A, :] = q2[s, j, A, :] + mr2[s, 1, 1].astype(F32) + sr2[s, 0].astype(F32)
        plus.wait_recv()
        final[s, B, :] = q2[s, j, B, :] + mr2[s, 0, 1].astype(F32) + sr2[s, 1].astype(F32)

    def output_group(g):
        top_row = lax.broadcasted_iota(jnp.int32, (8, 128), 0) == 0

        def column(fc, carry):
            pieces = []
            for tt in range(4):
                v0 = final[4 * g + tt, pl.ds(pl.multiple_of(8 * fc, 8), 8), :]
                v1 = final[4 * g + tt, pl.ds(pl.multiple_of(128 + 8 * fc, 8), 8), :]
                if tt % 2:
                    v0, v1 = jnp.where(top_row, v0, v1), jnp.where(top_row, v1, v0)
                pieces += [v0, v1]
            turned = jnp.concatenate(pieces, axis=0).T
            out_row = (fc // 2 * 2 + g) * 2 + fc % 2
            out_ref[pl.ds(out_row, 64, stride=32), :] = jnp.concatenate([turned[0:64], turned[64:128]], axis=1)
            return carry

        lax.fori_loop(0, 16, column, 0)

    stages = tuple(zip((compute, relay1, owner1, relay2, owner2), LAGS))
    last = FIRST + LAGS[-1] + 4

    def step(k, carry):
        @pl.when(k < 2)
        def _():
            pass_on(k)

        @pl.when((k == 0) | (k == STEP_A))
        def _():
            transform_group((k + STEP_A - 1) // STEP_A)

        @pl.when(k == 0)
        def _():
            for d, other in pairs:
                near(1, d, other).start()

        @pl.when((k == 1) | (k == STEP_B))
        def _():
            place_group((k + STEP_B - 2) // STEP_B)

        @pl.when((k == 2) | (k == STEP_C))
        def _():
            receive_group((k + STEP_C - 3) // STEP_C)

        for stage, lag in stages:
            start = FIRST + lag

            @pl.when(((k >= start) & (k < start + 4)) | ((k >= start + 4 + DELAY) & (k < start + 8 + DELAY)))
            def _():
                late = (k - start) // (4 + DELAY)
                stage(k - start - late * DELAY)

        @pl.when((k == last) | (k == last + 4 + DELAY))
        def _():
            output_group((k - last) // (4 + DELAY))

        return carry

    lax.fori_loop(0, last + 5 + DELAY, step, 0)

    def drain(s, carry):
        par = s % 2
        for kind, src, dst, axis in ((0, ms1, mr1, par), (1, ss1, sr1, par), (2, ms2, mr2, 1 - par), (3, ss2, sr2, 1 - par)):
            for copy in copies(s, kind, src, dst, axis):
                copy.wait_send()
        return carry

    lax.fori_loop(0, NBLOCK, drain, 0)

    def drain_group(g, carry):
        for d, other in pairs:
            far(g, d, other).wait_send()
            near(g, d, other).wait_send()
            forward(g, d, other).wait_send()
        side(g).wait_send()
        for dy, dc in order_peers:
            exchange_order(g, dy, dc).wait_send()
        for dx, dz in blk_peers:
            exchange_blk(g, dx, dz).wait_send()
        return carry

    lax.fori_loop(0, 2, drain_group, 0)


def analysis(field, mask, plan, legendre):
    high, low = dft_tables()
    vmem, anywhere = pl.BlockSpec(memory_space=pltpu.VMEM), pl.BlockSpec(memory_space=pl.ANY)
    dma = pltpu.SemaphoreType.DMA
    half = (NBLOCK, 2, 4, 128, 128)
    return pl.pallas_call(
        kernel,
        out_shape=jax.ShapeDtypeStruct((2048, 128), F32),
        in_specs=[anywhere, anywhere, vmem, anywhere, anywhere, anywhere, anywhere],
        out_specs=vmem,
        scratch_shapes=[
            pltpu.VMEM((16, 64, 512), F32),
            pltpu.VMEM((64, 512), jnp.int32),
            pltpu.VMEM((16, 128, 256), BF), pltpu.VMEM((16, 128, 256), BF), pltpu.VMEM((128, 128), BF),
            pltpu.VMEM((2, 8, 64, 512), F32),
            pltpu.VMEM((2, 2, 2, 32, 512), F32),
            pltpu.VMEM((16, 64, 512), BF),
            pltpu.VMEM((8, 8, 16, 128), BF),
            pltpu.VMEM((2, 8, 8, 16, 128), BF), pltpu.VMEM((2, 8, 8, 16, 128), BF),
            pltpu.VMEM((128, 128), BF), pltpu.VMEM((2, 2, 256, 768), BF),
            pltpu.VMEM((2, 16, 4, 16, 128), BF), pltpu.VMEM((2, 16, 4, 16, 128), BF),
            pltpu.VMEM((8, 48, 16, 1024), BF),
            pltpu.VMEM((4, 4, 4, 256, 128), F32),
            pltpu.VMEM((NBLOCK, 4, 256, 128), F32),
            pltpu.VMEM((NBLOCK, 2, 2, 4, 128, 128), BF), pltpu.VMEM((NBLOCK, 2, 2, 4, 128, 128), BF),
            pltpu.VMEM(half, BF), pltpu.VMEM(half, BF),
            pltpu.VMEM((NBLOCK, 2, 2, 128, 128), BF), pltpu.VMEM((NBLOCK, 2, 2, 128, 128), BF),
            pltpu.VMEM((NBLOCK, 2, 128, 128), BF), pltpu.VMEM((NBLOCK, 2, 128, 128), BF),
            pltpu.VMEM((NBLOCK, 256, 128), F32),
            dma((16,)), dma((4,)), dma((8,)),
            dma((2, 2, 2)), dma((2, 2, 2)), dma((2, 2, 2)), dma((2, 2, 2)), dma((2, 2, 2)), dma((2, 2, 2)),
            dma((2,)), dma((2,)), dma((2, 4, 2)), dma((2, 4, 2)), dma((2, 4, 4)), dma((2, 4, 4)),
            dma((NBLOCK, 4, 2)), dma((NBLOCK, 4, 2)),
        ],
        compiler_params=pltpu.CompilerParams(collective_id=0, has_side_effects=True, vmem_limit_bytes=62 * 2**20),
    )(field, mask, plan.reshape(16, 64), jnp.asarray(high), jnp.asarray(low), jnp.asarray(order_permutation()), legendre)


def body(field, ocean_mask, plan, legendre):
    return analysis(field, ocean_mask, plan, legendre).reshape(64, 16, 2, 128)


def solution(mesh):
    placed = (P(None, "blk", "order"), P("blk", "order"), P(), P("blk", "order", None))
    return jax.shard_map(
        body, mesh=mesh, in_specs=placed, out_specs=P("blk", None, None, "order"), check_vma=False
    )
```

time: 195 us -> 115 us (0.59)
  waiting for transfers between devices: 59 us -> 0 us
  Pallas kernels: 67.1 us -> 111 us
  matrix products: 19.6 us -> 0 us
  other arithmetic: 15.5 us -> 0 us
  between operations: 13.5 us -> 0.01 us
  starting transfers between devices: 8.21 us -> 0 us
  local copies, waits for them, and re-layouts: 11.3 us -> 3.62 us
    pallas_call x1, Pallas kernels: 67.1 us -> 111 us  [analysis(): pl.pallas_call(kernel, out_shape=jax.ShapeDtypeStruct((2048, 128), F32),...]
    reduce_scatter x1 -> x0, waiting for transfers between devices: 40.1 us -> none  [body(): lax.psum_scatter(terms, 'order', scatter_dimension=3, tiled=True)]
    dot_general x4 -> x0, matrix products: 19.6 us -> none  [the longest x1 13.4 us: transform(): jnp.einsum('frn,ncm->frcm', values, table, precision=lax.Precision.HIGHEST)]
    all_to_all x1 -> x0, waiting for transfers between devices: 18.9 us -> none  [pack_cycles(): lax.all_to_all(outgoing, 'blk', split_axis=1, concat_axis=1, tiled=True)]
    mul x2 -> x0, other arithmetic: 10.8 us -> none  [the longest x1 10.8 us: twiddle(): return jnp.stack([jnp.cos(angle) * scale, -jnp.sin(angle) * scale], axis=1)]
    all_to_all x1 -> x0, starting transfers between devices: 7.99 us -> none  [pack_cycles(): lax.all_to_all(outgoing, 'blk', split_axis=1, concat_axis=1, tiled=True)]
    reshape x3 -> x1, local copies, waits for them, and re-layouts: 6.83 us -> 1.35 us  [analysis(): plan.reshape(16, 64)]
    transpose x2 -> x0, local copies, waits for them, and re-layouts: 3.71 us -> none  [the longest x1 2.53 us: pack_cycles(): jnp.einsum('qr,frn->fqn', send_onehot, masked, precision=lax.Precision.HI...]
  transfers between devices with their start and end apart: 2 -> 0, of which waited for: 2 -> 0; matrix products, arithmetic and copies ran while one was open for 6% -> 0% of each run, Pallas kernels for 0% -> 0%
where the time goes in v3:
time: 115 us; the launch traced here: 114 us
  Pallas kernels  111 us (97%)
  local copies, waits for them, and re-layouts  3.62 us (3%)
    pallas_call x1, Pallas kernels, analysis(): pl.pallas_call(kernel, out_shape=jax.ShapeDtypeStruct((2048, 128), F32),...  111 us

profile of v3, /device:TPU:0, one launch (start us, length us, event | category | flops | bytes accessed | tf_op | source)
XLA Modules:
  0.0 114.5 jit_solution(835641145154864086)
XLA Ops:
  0.0 1.4 %reshape.6.plan_ref = s32[16,64]{1,0:T(8,128)} reshape(s32[1024]{0:T(1024)} %param.9) | data formatting | bytes 8192 | tf_op jit(solution)/shard_map/reshape | solution.py:539
  1.4 110.9 %shard_map.73 = f32[2048,128]{1,0:T(8,128)} custom-call(f32[16,64,512]{2,1,0:T(8,128)} %field_hbm.1, s32[64,512]{1,0:T(8,128)} %mask_hbm.1, s32[16,64]{1,0:T(8,128)} %reshape.6.plan_ref, bf16[16,128,256]{2,1,0:T(8,128)(2,1)} %constant.6.clone.high_hbm, bf16[16,128,256]{2,1,0:T(8,128)(2,1)} %constant.7.clone.low_hbm, ...), custom_call_target="tpu_custom_call" | custom-call | tf_op jit(solution)/shard_map/pallas_call | solution.py:509
  112.2 2.3 %copy.9 = f32[64,16,2,128]{3,2,1,0:T(2,128)} copy(f32[64,16,2,128]{3,2,1,0:T(2,128)} %bitcast.1) | data formatting | bytes 2097152

commit v4 on v3

v4 whole, which is shorter than its diff:
```python
import math

import jax
import jax.numpy as jnp
import numpy as np
from jax import lax
from jax.experimental import pallas as pl
from jax.experimental.pallas import tpu as pltpu
from jax.sharding import PartitionSpec as P

NLON = 4096
MESH = pl.DeviceIdType.MESH
BF = jnp.bfloat16
F32 = jnp.float32
NBLOCK = 8
CONTRACT_LANES = (((1,), (1,)), ((), ()))
CONTRACT_ROWS = (((0,), (0,)), ((), ()))

PIECES = 2
SPAN = 4 // PIECES
SCHEDULE = (
    "P0", "F1", "M0", "A0", "N1", "P1", "B00", "B01", "C00", "m0", "m1", "C01", "m2", "A1", "m3", "r0", "r1", "B10",
    "B11", "r2", "o0", "r3", "o1", "C10", "m4", "C11", "m5", "o2", "o3", "m6", "m7", "R0", "R1", "r4", "r5", "R2",
    "R3", "r6", "r7", "o4", "o5", "O0", "O1", "O2", "O3", "T0", "R4", "o6", "R5", "o7", "D", "R6", "R7", "O4", "O5",
    "O6", "O7", "T1", "E",
)


def dft_tables():
    r = np.arange(16)[:, None, None]
    column = np.arange(64)[None, :, None]
    owner, w, ql = column // 8, column // 4 % 2, column % 4
    residue = np.where(w == 0, r, np.where(r == 0, 16, 32 - r))
    m = 32 * (4 * owner + ql) + residue
    i = np.arange(128)[None, None, :]
    angle = 2.0 * np.pi * (m * i % NLON) / NLON
    real, imag = np.cos(angle) / 64.0, np.where(w == 0, 1.0, -1.0) * np.sin(angle) / 64.0
    table = np.concatenate([real, imag], axis=2).astype(np.float32)
    high = table.astype(jnp.bfloat16)
    low = (table - high.astype(np.float32)).astype(jnp.bfloat16)
    return high, low


def order_permutation():
    out = np.zeros((128, 128), np.float32)
    for r in range(8):
        for w in range(2):
            for c in range(2):
                for ql in range(4):
                    mh = r if w == 0 else (8 - r) % 8
                    t = 2 * ql + w
                    out[(t % 4 * 2 + t // 4) * 16 + c * 8 + mh, r * 16 + c * 8 + w * 4 + ql] = 1.0
    return out.astype(jnp.bfloat16)


def real_dft(values):
    n = len(values)
    if n == 2:
        return [(values[0] + values[1], None), (values[0] - values[1], None)]
    even, odd = real_dft(values[0::2]), real_dft(values[1::2])
    half = n // 2

    def term(part, k):
        if k <= half // 2:
            return part[k]
        re, im = part[half - k]
        return re, (None if im is None else -im)

    result = [None] * (half + 1)
    for k in range(half // 2 + 1):
        er, ei = even[k]
        qr, qi = odd[k]
        cos, sin = math.cos(2 * math.pi * k / n), math.sin(2 * math.pi * k / n)
        if k == 0:
            result[0] = (er + qr, None)
            result[half] = (er - qr, None)
            continue
        if 4 * k == n:
            tr, ti = qi, -qr
        else:
            tr = qr * cos + qi * sin if qi is not None else qr * cos
            ti = qi * cos - qr * sin if qi is not None else -(qr * sin)

        def add(a, b, sign):
            if a is None:
                return None if b is None else (b if sign > 0 else -b)
            if b is None:
                return a
            return a + b if sign > 0 else a - b

        result[k] = (add(er, tr, 1), add(ei, ti, 1))
        if k != half - k:
            ni = add(ei, ti, -1)
            result[half - k] = (add(er, tr, -1), None if ni is None else -ni)
    return result


def kernel(field_hbm, mask_hbm, plan_ref, high_hbm, low_hbm, perm_hbm, leg_hbm, out_ref,
           masked, mask, table, perm, xr, relay, ycat, terms, sbuf, srecv, place, expand, sent, arrived,
           leg, q, q2, ms1, mr1, ss1, sr1, ms2, mr2, ss2, sr2, final,
           field_sem, load_sem, leg_sem, far_s, far_r, near_s, near_r, fwd_s, fwd_r, side_s, side_r,
           ox_s, ox_r, bx_s, bx_r, ring_s, ring_r):
    order = lax.axis_index("order")
    y, core = order // 2, order % 2
    me = lax.axis_index("blk")
    x, z = me // 4, me % 4

    def load_field(g, o):
        f = 2 * o + g
        return pltpu.make_async_copy(field_hbm.at[f], masked.at[f], field_sem.at[g])

    loads = [pltpu.make_async_copy(src, dst, load_sem.at[i]) for i, (src, dst) in enumerate(
        ((mask_hbm, mask), (high_hbm, table.at[:, pl.ds(0, 64), 0:256]),
         (low_hbm, table.at[:, pl.ds(0, 64), 512:768]), (perm_hbm, perm)))]

    def load_leg(t):
        return pltpu.make_async_copy(leg_hbm.at[:, pl.ds(16 * t, 16), :], leg.at[t // 4, t % 4], leg_sem.at[t % 4])

    loads[0].start()
    for o in range(8):
        load_field(0, o).start()

    barrier = pltpu.get_barrier_semaphore()
    order_peers = [(dy, dc) for dy in range(4) for dc in range(2) if (dy, dc) != (0, 0)]
    blk_peers = [(dx, dz) for dx in range(4) for dz in range(4) if (dx, dz) != (0, 0)]

    def at(dy, other):
        return {"order": (y + dy) % 4 * 2 + other}

    for dy, dc in order_peers:
        pl.semaphore_signal(barrier, inc=1, device_id=at(dy, (core + dc) % 2), device_id_type=MESH)
    for dx, dz in blk_peers:
        pl.semaphore_signal(barrier, inc=1, device_id={"blk": (x + dx) % 4 * 4 + (z + dz) % 4}, device_id_type=MESH)

    for o in range(8):
        load_field(1, o).start()
    for copy in loads[1:]:
        copy.start()
    loads[0].wait()

    def mask_fields(g):
        pltpu.make_async_copy(field_hbm.at[pl.ds(0, 8)], masked.at[pl.ds(0, 8)], field_sem.at[g]).wait()

        def one(o, carry):
            masked[2 * o + g] = masked[2 * o + g] * mask[...].astype(F32)
            return carry

        lax.fori_loop(0, 8, one, 0)
        xr[g, order] = masked[order * 2 + g]

    def remote(src, dst, ss, rs, device):
        return pltpu.make_async_remote_copy(src_ref=src, dst_ref=dst, send_sem=ss, recv_sem=rs,
                                            device_id=device, device_id_type=MESH)

    halves = (pl.ds(0, 32), pl.ds(32, 32))
    steps = (1, 3)
    pairs = [(d, other) for d in range(2) for other in range(2)]

    def far(g, d, other):
        target = ((y + 2) % 4 * 2 + other) * 2 + g
        return remote(masked.at[target, halves[d]], relay.at[g, d, core], far_s.at[g], far_r.at[g, d, core],
                      at(steps[d], other))

    def near(g, d, other):
        target = ((y + steps[d]) % 4 * 2 + other) * 2 + g
        return remote(masked.at[target], xr.at[g, order], near_s.at[g], near_r.at[g],
                      at(steps[d], other))

    def forward(g, d, source):
        origin = (y + 4 - steps[d]) % 4 * 2 + source
        return remote(relay.at[g, d, source], xr.at[g, origin, halves[d]], fwd_s.at[g], fwd_r.at[g],
                      at(steps[d], core))

    def side(g):
        target = (y * 2 + 1 - core) * 2 + g
        return remote(masked.at[target], xr.at[g, order], side_s.at[g], side_r.at[g], at(0, 1 - core))

    def wait_far(g, d, source):
        remote(masked.at[0, halves[d]], relay.at[g, d, source], far_s.at[g], far_r.at[g, d, source],
               at(steps[d], source)).wait_recv()

    def all_far(g):
        return remote(relay.at[g], relay.at[g], far_s.at[g], far_r.at[g, 0, 0], at(1, 0))

    def all_near(g):
        part = pl.ds(0, 4)
        return remote(xr.at[g, part], xr.at[g, part], near_s.at[g], near_r.at[g], at(1, 0))

    def all_forward(g):
        return remote(relay.at[g], relay.at[g], fwd_s.at[g], fwd_r.at[g], at(1, 0))

    mask_fields(0)
    pl.semaphore_wait(barrier, 22)
    for d, other in pairs:
        far(0, d, other).start()
    for d, other in pairs:
        near(0, d, other).start()
    side(0).start()
    for t in range(8):
        load_leg(t).start()
    mask_fields(1)
    side(1).start()

    earlier = (lax.broadcasted_iota(jnp.int32, (64, 64), 0) < lax.broadcasted_iota(jnp.int32, (64, 64), 1))
    earlier = earlier.astype(F32).astype(BF)

    def owner_of(b, rows):
        both = plan_ref[pl.ds(b // 2, 1), :]
        slots = jnp.broadcast_to(jnp.where(b % 2 == 0, both[:, 0:64], both[:, 64:128]), (rows, 64))
        owner = jnp.zeros((rows, 64), jnp.int32)
        for b in range(1, 17):
            owner += (slots >= 48 * b).astype(jnp.int32)
        return slots, owner

    def source_maps(_):
        row = lax.broadcasted_iota(jnp.int32, (128, 64), 0)
        _, owner = owner_of(me, 128)
        mine = owner == row // 8
        count = jnp.dot(mine.astype(F32).astype(BF), earlier, preferred_element_type=F32)
        match = mine & (count == (row // 2 % 4).astype(F32))
        for rh in range(2):
            place[:, 64 * rh:64 * rh + 64] = (match & (row % 2 == rh)).astype(F32).astype(BF)

        def source_map(b, carry):
            slots, owner = owner_of(b, 16)
            mine = owner == me
            count = jnp.dot(mine.astype(F32).astype(BF), earlier, preferred_element_type=F32)
            rows = lax.broadcasted_iota(jnp.int32, (16, 64), 0)
            match = mine & (count == (rows // 2 % 4).astype(F32))
            slot = jnp.sum(jnp.where(match, (slots - 48 * me + 1).astype(F32), 0.0), axis=1, keepdims=True)
            lanes = lax.broadcasted_iota(jnp.int32, (16, 768), 1) // 16 + 1
            rows = lax.broadcasted_iota(jnp.int32, (16, 768), 0)
            hit = jnp.broadcast_to(slot, (16, 768)) == lanes.astype(F32)
            for h in range(2):
                for rh in range(2):
                    expand[h, rh, pl.ds(pl.multiple_of(16 * b, 16), 16), :] = (
                        hit & (rows // 8 == h) & (rows % 2 == rh)).astype(F32).astype(BF)
            return carry

        lax.fori_loop(0, 16, source_map, 0)
        for copy in loads[1:]:
            copy.wait()

        w = lax.broadcasted_iota(jnp.int32, (64, 128), 0) // 4 % 2

        def complete(r, carry):
            for start in (0, 512):
                real = table[r, 0:64, start:start + 128].astype(F32)
                imag = table[r, 0:64, start + 128:start + 256].astype(F32)
                sign = jnp.where(w == 0, 1.0, -1.0)
                special = jnp.broadcast_to(r == 0, (64, 128))
                parts = (
                    (jnp.where(special & (w == 1), 0.0, real), jnp.where(special, jnp.where(w == 1, real, 0.0), imag)),
                    (jnp.where(special & (w == 1), 0.0, -sign * imag),
                     jnp.where(special, jnp.where(w == 1, imag, 0.0), sign * real)),
                )
                for c in range(2):
                    for half in range(2):
                        value = parts[c][half].astype(BF)
                        table[r, 64 * c:64 * c + 64, start + 128 * half:start + 128 * half + 128] = value
                        if start == 0:
                            table[r, 64 * c:64 * c + 64, 256 + 128 * half:384 + 128 * half] = value
            return carry

        lax.fori_loop(0, 16, complete, 0)

    def exchange_order(g, piece, peer):
        target = (y + peer // 2) % 4 * 2 + (core + peer) % 2
        rows = pl.ds(2 * SPAN * piece, 2 * SPAN)
        return remote(sbuf.at[g, target, rows], srecv.at[g, order, rows], ox_s.at[g, piece], ox_r.at[g, piece],
                      {"order": target})

    def exchange_blk(g, piece, peer):
        target = (x + peer // 4) % 4 * 4 + (z + peer) % 4
        rows = pl.ds(SPAN * piece, SPAN)
        return remote(sent.at[g, target, rows], arrived.at[g, me, rows], bx_s.at[g, piece], bx_r.at[g, piece],
                      {"blk": target})

    def all_order(g, piece):
        part = srecv.at[g, pl.ds(0, 7), pl.ds(2 * SPAN * piece, 2 * SPAN)]
        return remote(part, part, ox_s.at[g, piece], ox_r.at[g, piece], at(1, 0))

    def all_blk(g, piece):
        part = arrived.at[g, pl.ds(0, 15), pl.ds(SPAN * piece, SPAN)]
        return remote(part, part, bx_s.at[g, piece], bx_r.at[g, piece], {"blk": (me + 1) % 16})

    order_first = (4, 5, 2, 3, 6, 7, 1)
    blk_first = (10, 9, 11, 6, 14, 8, 2, 5, 7, 13, 15, 1, 3, 4, 12)

    def pass_on(g):
        for d, source in pairs:
            wait_far(g, d, source)
            forward(g, d, source).start()

    def transform_group(g):
        all_near(g).wait_recv()
        side(g).wait_recv()
        all_forward(g).wait_recv()

        def butterfly(k, carry):
            rows = pl.ds(pl.multiple_of(16 * k, 16), 16)
            values = [xr[g, a // 4, rows, 128 * (a % 4):128 * (a % 4) + 128] for a in range(32)]
            result = real_dft(values)
            for r in range(16):
                pair = (result[0][0], result[16][0]) if r == 0 else result[r]
                for part, value in enumerate(pair):
                    top = value.astype(BF)
                    ycat[r, rows, 128 * part:128 * part + 128] = top
                    ycat[r, rows, 256 + 128 * part:384 + 128 * part] = (value - top.astype(F32)).astype(BF)
                    ycat[r, rows, 512 + 128 * part:640 + 128 * part] = top
            return carry

        lax.fori_loop(0, 4, butterfly, 0)

        for r in range(8):
            parts = [lax.dot_general(table[rr], ycat[rr], CONTRACT_LANES, preferred_element_type=F32) for rr in (r, r + 8)]
            both = jnp.concatenate(parts, axis=1)
            for o in range(8):
                rows = jnp.concatenate([both[8 * o:8 * o + 8], both[64 + 8 * o:64 + 8 * o + 8]], axis=0)
                terms[16 * r:16 * r + 16, 128 * o:128 * o + 128] = rows.astype(BF)
        part = jnp.dot(perm[...], terms[...], preferred_element_type=F32).astype(BF)
        for o in range(8):
            sbuf[g, o] = part[:, 128 * o:128 * o + 128].reshape(8, 16, 128)
        for piece in range(PIECES):
            for peer in order_first:
                exchange_order(g, piece, peer).start()
        srecv[g, order] = sbuf[g, order]

    def place_group(g, piece):
        all_order(g, piece).wait_recv()
        for tt in range(SPAN * piece, SPAN * piece + SPAN):
            parts = []
            for h in range(2):
                rows = srecv[g, :, 2 * tt + h].reshape(128, 128)
                out = lax.dot_general(place[...], rows, CONTRACT_LANES, preferred_element_type=F32)
                parts.append(out.reshape(16, 8, 128))
            sent[g, :, tt] = jnp.concatenate(parts, axis=1).astype(BF)
            arrived[g, me, tt] = sent[g, me, tt]
        for peer in blk_first:
            exchange_blk(g, piece, peer).start()

    def receive_group(g, piece):
        all_blk(g, piece).wait_recv()

    low_lanes = lax.broadcasted_iota(jnp.int32, (256, 128), 1) < 64

    def neighbour(axis, step):
        nx = (x + step * (1 - axis)) % 4
        nz = (z + step * axis) % 4
        return {"blk": nx * 4 + nz}

    def copies(s, kind, src, dst, axis):
        return [remote(src.at[s, way], dst.at[s, way], ring_s.at[s, kind], ring_r.at[s, kind],
                       neighbour(axis, 3 - 2 * way)) for way in range(2)]

    def ring(s, kind, src, dst):
        return remote(src.at[s], dst.at[s], ring_s.at[s, kind], ring_r.at[s, kind], {"blk": (me + 1) % 16})

    A, B = pl.ds(0, 128), pl.ds(128, 128)

    def compute(s):
        g, tt, par, qs = s // 4, s % 4, s % 2, s % 4

        if s < 4:
            pltpu.make_async_copy(leg.at[:, tt], leg.at[:, tt], leg_sem.at[tt]).wait()

        rows = lax.broadcasted_iota(jnp.int32, (256, 768), 0)
        lanes = lax.broadcasted_iota(jnp.int32, (256, 768), 1) % 16
        rh, mh = rows // 128, rows % 8
        swapped = (par == 1) & (mh > 0)
        mask = lanes == jnp.where(swapped, 8 - 8 * rh, 8 * rh) + mh
        values = arrived[g, :, tt].reshape(256, 128)
        lhs = []
        for h in range(2):
            ex = jnp.concatenate([
                lax.dot_general(values, expand[h, part], CONTRACT_ROWS, preferred_element_type=F32)
                for part in range(2)], axis=0)
            lhs.append(jnp.where(mask, ex, 0.0).astype(BF))
        for bx in range(4):
            pa, pb = [
                jnp.dot(lhs[h], leg[h, tt, :, :, 256 * bx:256 * bx + 256].reshape(768, 256),
                        preferred_element_type=F32)
                for h in range(2)
            ]
            for half in range(2):
                a = pa[:, 128 * half:128 * half + 128]
                b = pb[:, 128 * half:128 * half + 128]
                first = jnp.where(low_lanes, a, pltpu.roll(b, 64, 1))
                second = jnp.where(low_lanes, pltpu.roll(a, 64, 1), b)
                for bz, value in ((2 * half, first), (2 * half + 1, second)):
                    q[qs, bx * (1 - par) + bz * par, bz * (1 - par) + bx * par] = value
        i = x * (1 - par) + z * par
        c1, c2, c3 = (i + 1) % 4, (i + 2) % 4, (i + 3) % 4
        minus, plus = copies(s, 0, ms1, mr1, par)
        ms1[s, 0, 0] = q[qs, c2, :, A, :].astype(BF)
        ms1[s, 0, 1] = q[qs, c3, :, B, :].astype(BF)
        minus.start()
        ms1[s, 1, 0] = q[qs, c2, :, B, :].astype(BF)
        ms1[s, 1, 1] = q[qs, c1, :, A, :].astype(BF)
        plus.start()

    def relay1(s):
        par, qs = s % 2, s % 4
        i = x * (1 - par) + z * par
        c1, c3 = (i + 1) % 4, (i + 3) % 4
        send = copies(s, 1, ss1, sr1, par)
        ring(s, 0, ms1, mr1).wait_recv()
        ss1[s, 0] = (q[qs, c3, :, A, :] + mr1[s, 0, 0].astype(F32)).astype(BF)
        send[0].start()
        ss1[s, 1] = (q[qs, c1, :, B, :] + mr1[s, 1, 0].astype(F32)).astype(BF)
        send[1].start()

    def owner1(s):
        par, qs = s % 2, s % 4
        i = x * (1 - par) + z * par
        ring(s, 1, ss1, sr1).wait_recv()
        q2[s, :, A, :] = q[qs, i, :, A, :] + mr1[s, 1, 1].astype(F32) + sr1[s, 0].astype(F32)
        q2[s, :, B, :] = q[qs, i, :, B, :] + mr1[s, 0, 1].astype(F32) + sr1[s, 1].astype(F32)
        j = z * (1 - par) + x * par
        d1, d2, d3 = (j + 1) % 4, (j + 2) % 4, (j + 3) % 4
        ms2[s, 0, 0] = q2[s, d2, A, :].astype(BF)
        ms2[s, 0, 1] = q2[s, d3, B, :].astype(BF)
        ms2[s, 1, 0] = q2[s, d2, B, :].astype(BF)
        ms2[s, 1, 1] = q2[s, d1, A, :].astype(BF)
        for copy in copies(s, 2, ms2, mr2, 1 - par):
            copy.start()

    def relay2(s):
        par = s % 2
        j = z * (1 - par) + x * par
        d1, d3 = (j + 1) % 4, (j + 3) % 4
        send = copies(s, 3, ss2, sr2, 1 - par)
        ring(s, 2, ms2, mr2).wait_recv()
        ss2[s, 0] = (q2[s, d3, A, :] + mr2[s, 0, 0].astype(F32)).astype(BF)
        send[0].start()
        ss2[s, 1] = (q2[s, d1, B, :] + mr2[s, 1, 0].astype(F32)).astype(BF)
        send[1].start()

    def owner2(s):
        par = s % 2
        j = z * (1 - par) + x * par
        ring(s, 3, ss2, sr2).wait_recv()
        final[s, A, :] = q2[s, j, A, :] + mr2[s, 1, 1].astype(F32) + sr2[s, 0].astype(F32)
        final[s, B, :] = q2[s, j, B, :] + mr2[s, 0, 1].astype(F32) + sr2[s, 1].astype(F32)

    def output_group(g):
        top_row = lax.broadcasted_iota(jnp.int32, (8, 128), 0) == 0

        def column(fc, carry):
            pieces = []
            for tt in range(4):
                v0 = final[4 * g + tt, pl.ds(pl.multiple_of(8 * fc, 8), 8), :]
                v1 = final[4 * g + tt, pl.ds(pl.multiple_of(128 + 8 * fc, 8), 8), :]
                if tt % 2:
                    v0, v1 = jnp.where(top_row, v0, v1), jnp.where(top_row, v1, v0)
                pieces += [v0, v1]
            turned = jnp.concatenate(pieces, axis=0).T
            out_row = (fc // 2 * 2 + g) * 2 + fc % 2
            out_ref[pl.ds(out_row, 64, stride=32), :] = jnp.concatenate([turned[0:64], turned[64:128]], axis=1)
            return carry

        lax.fori_loop(0, 16, column, 0, unroll=4)

    def near_group(g):
        for d, other in pairs:
            near(g, d, other).start()

    def far_group(g):
        for d, other in pairs:
            far(g, d, other).start()

    def ring_drain(s, kinds):
        for kind in kinds:
            src, dst = ((ms1, mr1), (ss1, sr1), (ms2, mr2), (ss2, sr2))[kind]
            ring(s, kind, src, dst).wait_send()

    def drain_early():
        for g in range(2):
            all_far(g).wait_send()
            all_near(g).wait_send()
            all_forward(g).wait_send()
            side(g).wait_send()
            for piece in range(PIECES):
                all_order(g, piece).wait_send()
                all_blk(g, piece).wait_send()
        for s in range(4):
            ring_drain(s, (0, 1, 2, 3))
        for s in range(4, 8):
            ring_drain(s, (0,))

    def drain_late():
        for s in range(4, 8):
            ring_drain(s, (1, 2, 3))

    run = dict(F=far_group, N=near_group, P=pass_on, A=transform_group, B=place_group, C=receive_group, M=source_maps,
               m=compute, r=relay1, o=owner1, R=relay2, O=owner2, T=output_group, D=drain_early, E=drain_late)
    for name in SCHEDULE:
        run[name[0]](*map(int, name[1:]))


def analysis(field, mask, plan, legendre):
    high, low = dft_tables()
    vmem, anywhere = pl.BlockSpec(memory_space=pltpu.VMEM), pl.BlockSpec(memory_space=pl.ANY)
    dma = pltpu.SemaphoreType.DMA
    half = (NBLOCK, 2, 4, 128, 128)
    return pl.pallas_call(
        kernel,
        out_shape=jax.ShapeDtypeStruct((2048, 128), F32),
        in_specs=[anywhere, anywhere, vmem, anywhere, anywhere, anywhere, anywhere],
        out_specs=vmem,
        scratch_shapes=[
            pltpu.VMEM((16, 64, 512), F32),
            pltpu.VMEM((64, 512), jnp.int32),
            pltpu.VMEM((16, 128, 768), BF), pltpu.VMEM((128, 128), BF),
            pltpu.VMEM((2, 8, 64, 512), F32),
            pltpu.VMEM((2, 2, 2, 32, 512), F32),
            pltpu.VMEM((16, 64, 768), BF),
            pltpu.VMEM((128, 1024), BF),
            pltpu.VMEM((2, 8, 8, 16, 128), BF), pltpu.VMEM((2, 8, 8, 16, 128), BF),
            pltpu.VMEM((128, 128), BF), pltpu.VMEM((2, 2, 256, 768), BF),
            pltpu.VMEM((2, 16, 4, 16, 128), BF), pltpu.VMEM((2, 16, 4, 16, 128), BF),
            pltpu.VMEM((2, 4, 48, 16, 1024), BF),
            pltpu.VMEM((4, 4, 4, 256, 128), F32),
            pltpu.VMEM((NBLOCK, 4, 256, 128), F32),
            pltpu.VMEM((NBLOCK, 2, 2, 4, 128, 128), BF), pltpu.VMEM((NBLOCK, 2, 2, 4, 128, 128), BF),
            pltpu.VMEM(half, BF), pltpu.VMEM(half, BF),
            pltpu.VMEM((NBLOCK, 2, 2, 128, 128), BF), pltpu.VMEM((NBLOCK, 2, 2, 128, 128), BF),
            pltpu.VMEM((NBLOCK, 2, 128, 128), BF), pltpu.VMEM((NBLOCK, 2, 128, 128), BF),
            pltpu.VMEM((NBLOCK, 256, 128), F32),
            dma((2,)), dma((4,)), dma((4,)),
            dma((2,)), dma((2, 2, 2)), dma((2,)), dma((2,)), dma((2,)), dma((2,)), dma((2,)), dma((2,)),
            dma((2, PIECES)), dma((2, PIECES)), dma((2, PIECES)), dma((2, PIECES)),
            dma((NBLOCK, 4)), dma((NBLOCK, 4)),
        ],
        compiler_params=pltpu.CompilerParams(collective_id=0, has_side_effects=True, vmem_limit_bytes=62 * 2**20),
    )(field, mask, plan.reshape(8, 128), jnp.asarray(high), jnp.asarray(low), jnp.asarray(order_permutation()), legendre)


def body(field, ocean_mask, plan, legendre):
    return analysis(field, ocean_mask, plan, legendre).reshape(64, 16, 2, 128)


def solution(mesh):
    placed = (P(None, "blk", "order"), P("blk", "order"), P(), P("blk", "order", None))
    return jax.shard_map(
        body, mesh=mesh, in_specs=placed, out_specs=P("blk", None, None, "order"), check_vma=False
    )
```

time: 115 us -> 95.2 us (0.83)
  Pallas kernels: 111 us -> 92.7 us
  local copies, waits for them, and re-layouts: 3.62 us -> 2.26 us
    pallas_call x1, Pallas kernels: 111 us -> 92.7 us  [analysis(): pl.pallas_call(kernel, out_shape=jax.ShapeDtypeStruct((2048, 128), F32),...]
    reshape x1 -> x0, local copies, waits for them, and re-layouts: 1.35 us -> none  [analysis(): plan.reshape(16, 64)]
where the time goes in v4:
time: 95.2 us; the launch traced here: 94.9 us
  Pallas kernels  92.7 us (97%)
  local copies, waits for them, and re-layouts  2.26 us (2%)
    pallas_call x1, Pallas kernels, analysis(): pl.pallas_call(kernel, out_shape=jax.ShapeDtypeStruct((2048, 128), F32),...  92.7 us
    unnamed x1, local copies, waits for them, and re-layouts  2.26 us

profile of v4, /device:TPU:0, one launch (start us, length us, event | category | flops | bytes accessed | tf_op | source)
XLA Modules:
  0.0 94.9 jit_solution(13115555851392636256)
XLA Ops:
  0.0 92.7 %shard_map.73 = f32[2048,128]{1,0:T(8,128)} custom-call(f32[16,64,512]{2,1,0:T(8,128)} %field_hbm.1, s32[64,512]{1,0:T(8,128)} %mask_hbm.1, s32[8,128]{1,0:T(8,128)} %bitcast.3, bf16[16,64,256]{2,1,0:T(8,128)(2,1)} %constant.6.clone.high_hbm, bf16[16,64,256]{2,1,0:T(8,128)(2,1)} %constant.7.clone.low_hbm, bf16[128,128]{1,0:T(8,128)(2,1)} %constant.8.clone.perm_hbm, ...), custom_call_target="tpu_custom_call" | custom-call | tf_op jit(solution)/shard_map/pallas_call | solution.py:506
  92.7 2.3 %copy.9 = f32[64,16,2,128]{3,2,1,0:T(2,128)} copy(f32[64,16,2,128]{3,2,1,0:T(2,128)} %bitcast.2) | data formatting | bytes 2097152

commit v5 on v4

--- a/solution.py
+++ b/solution.py
@@ -19,9 +19,9 @@
 PIECES = 2
 SPAN = 4 // PIECES
 SCHEDULE = (
-    "P0", "F1", "M0", "A0", "N1", "P1", "B00", "B01", "C00", "m0", "m1", "C01", "m2", "A1", "m3", "r0", "r1", "B10",
-    "B11", "r2", "o0", "r3", "o1", "C10", "m4", "C11", "m5", "o2", "o3", "m6", "m7", "R0", "R1", "r4", "r5", "R2",
-    "R3", "r6", "r7", "o4", "o5", "O0", "O1", "O2", "O3", "T0", "R4", "o6", "R5", "o7", "D", "R6", "R7", "O4", "O5",
+    "P0", "F1", "M0", "A0", "N1", "P1", "B00", "B01", "C00", "m0", "m1", "C01", "A1", "m2", "m3", "r0", "B10", "B11",
+    "r1", "r2", "o0", "r3", "o1", "C10", "m4", "C11", "m5", "o2", "m6", "o3", "m7", "R0", "R1", "r4", "r5", "R2",
+    "R3", "r6", "r7", "o4", "o5", "O0", "O1", "O2", "O3", "T0", "o6", "o7", "R4", "R5", "D", "R6", "R7", "O4", "O5",
     "O6", "O7", "T1", "E",
 )
 
@@ -505,7 +505,7 @@
     half = (NBLOCK, 2, 4, 128, 128)
     return pl.pallas_call(
         kernel,
-        out_shape=jax.ShapeDtypeStruct((2048, 128), F32),
+        out_shape=pltpu.VMEM((2048, 128), F32),
         in_specs=[anywhere, anywhere, vmem, anywhere, anywhere, anywhere, anywhere],
         out_specs=vmem,
         scratch_shapes=[

time: 95.2 us -> 91.5 us (0.961)
  Pallas kernels: 92.7 us -> 90.2 us
  local copies, waits for them, and re-layouts: 2.26 us -> 0.97 us
    pallas_call x1, Pallas kernels: 92.7 us -> 90.2 us  [analysis(): pl.pallas_call(kernel, out_shape=pltpu.VMEM((2048, 128), F32), in_specs=[...]
    unnamed x1, local copies, waits for them, and re-layouts: 2.26 us -> 0.97 us
where the time goes in v5:
time: 91.5 us; the launch traced here: 91.2 us
  Pallas kernels  90.2 us (99%)
  local copies, waits for them, and re-layouts  0.97 us (1%)
    pallas_call x1, Pallas kernels, analysis(): pl.pallas_call(kernel, out_shape=pltpu.VMEM((2048, 128), F32), in_specs=[...  90.2 us

profile of v5, /device:TPU:0, one launch (start us, length us, event | category | flops | bytes accessed | tf_op | source)
XLA Modules:
  0.0 91.2 jit_solution(8196833007482242686)
XLA Ops:
  0.0 90.2 %shard_map.73 = f32[2048,128]{1,0:T(8,128)S(1)} custom-call(f32[16,64,512]{2,1,0:T(8,128)} %field_hbm.1, s32[64,512]{1,0:T(8,128)} %mask_hbm.1, s32[8,128]{1,0:T(8,128)} %bitcast.3, bf16[16,64,256]{2,1,0:T(8,128)(2,1)} %constant.6.clone.high_hbm, bf16[16,64,256]{2,1,0:T(8,128)(2,1)} %constant.7.clone.low_hbm, bf16[128,128]{1,0:T(8,128)(2,1)} %constant.8.clone.perm_hbm, ...), custom_call_target="tpu_custom_call" | custom-call | tf_op jit(solution)/shard_map/pallas_call | solution.py:506
  90.3 1.0 %copy.9 = f32[64,16,2,128]{3,2,1,0:T(2,128)} copy(f32[64,16,2,128]{3,2,1,0:T(2,128)S(1)} %bitcast.2) | data formatting | bytes 2097152

commit v6 on v5

--- a/solution.py
+++ b/solution.py
@@ -18,11 +18,12 @@
 
 PIECES = 2
 SPAN = 4 // PIECES
+DIRECT = (6, 7)
 SCHEDULE = (
     "P0", "F1", "M0", "A0", "N1", "P1", "B00", "B01", "C00", "m0", "m1", "C01", "A1", "m2", "m3", "r0", "B10", "B11",
     "r1", "r2", "o0", "r3", "o1", "C10", "m4", "C11", "m5", "o2", "m6", "o3", "m7", "R0", "R1", "r4", "r5", "R2",
-    "R3", "r6", "r7", "o4", "o5", "O0", "O1", "O2", "O3", "T0", "o6", "o7", "R4", "R5", "D", "R6", "R7", "O4", "O5",
-    "O6", "O7", "T1", "E",
+    "R3", "r6", "r7", "o4", "o5", "O0", "O1", "O2", "O3", "T0", "o6", "o7", "R4", "R5", "D", "O4", "O5", "O6", "O7",
+    "T1", "E",
 )
 
 
@@ -418,6 +419,14 @@
         q2[s, :, B, :] = q[qs, i, :, B, :] + mr1[s, 0, 1].astype(F32) + sr1[s, 1].astype(F32)
         j = z * (1 - par) + x * par
         d1, d2, d3 = (j + 1) % 4, (j + 2) % 4, (j + 3) % 4
+        if s in DIRECT:
+            ss2[s] = q2[s, d2].reshape(2, 128, 128).astype(BF)
+            remote(ss2.at[s], sr2.at[s], ring_s.at[s, 3], ring_r.at[s, 3], neighbour(1 - par, 2)).start()
+            ms2[s, 0] = q2[s, d3].reshape(2, 128, 128).astype(BF)
+            ms2[s, 1] = q2[s, d1].reshape(2, 128, 128).astype(BF)
+            for copy in copies(s, 2, ms2, mr2, 1 - par):
+                copy.start()
+            return
         ms2[s, 0, 0] = q2[s, d2, A, :].astype(BF)
         ms2[s, 0, 1] = q2[s, d3, B, :].astype(BF)
         ms2[s, 1, 0] = q2[s, d2, B, :].astype(BF)
@@ -439,6 +448,12 @@
     def owner2(s):
         par = s % 2
         j = z * (1 - par) + x * par
+        if s in DIRECT:
+            ring(s, 2, ms2, mr2).wait_recv()
+            ring(s, 3, ss2, sr2).wait_recv()
+            total = mr2[s, 0].astype(F32) + mr2[s, 1].astype(F32) + sr2[s].astype(F32)
+            final[s] = q2[s, j] + total.reshape(256, 128)
+            return
         ring(s, 3, ss2, sr2).wait_recv()
         final[s, A, :] = q2[s, j, A, :] + mr2[s, 1, 1].astype(F32) + sr2[s, 0].astype(F32)
         final[s, B, :] = q2[s, j, B, :] + mr2[s, 0, 1].astype(F32) + sr2[s, 1].astype(F32)
@@ -459,7 +474,7 @@
             out_ref[pl.ds(out_row, 64, stride=32), :] = jnp.concatenate([turned[0:64], turned[64:128]], axis=1)
             return carry
 
-        lax.fori_loop(0, 16, column, 0, unroll=4)
+        lax.fori_loop(0, 16, column, 0, unroll=16)
 
     def near_group(g):
         for d, other in pairs:

time: 91.5 us -> 89.3 us (0.976)
  Pallas kernels: 90.2 us -> 88.1 us
    pallas_call x1, Pallas kernels: 90.2 us -> 88.1 us  [analysis(): pl.pallas_call(kernel, out_shape=pltpu.VMEM((2048, 128), F32), in_specs=[...]
where the time goes in v6:
time: 89.3 us; the launch traced here: 89.1 us
  Pallas kernels  88.1 us (99%)
  local copies, waits for them, and re-layouts  0.97 us (1%)
    pallas_call x1, Pallas kernels, analysis(): pl.pallas_call(kernel, out_shape=pltpu.VMEM((2048, 128), F32), in_specs=[...  88.1 us

profile of v6, /device:TPU:0, one launch (start us, length us, event | category | flops | bytes accessed | tf_op | source)
XLA Modules:
  0.0 89.1 jit_solution(1251782294043176941)
XLA Ops:
  0.0 88.1 %shard_map.73 = f32[2048,128]{1,0:T(8,128)S(1)} custom-call(f32[16,64,512]{2,1,0:T(8,128)} %field_hbm.1, s32[64,512]{1,0:T(8,128)} %mask_hbm.1, s32[8,128]{1,0:T(8,128)} %bitcast.3, bf16[16,64,256]{2,1,0:T(8,128)(2,1)} %constant.6.clone.high_hbm, bf16[16,64,256]{2,1,0:T(8,128)(2,1)} %constant.7.clone.low_hbm, bf16[128,128]{1,0:T(8,128)(2,1)} %constant.8.clone.perm_hbm, ...), custom_call_target="tpu_custom_call" | custom-call | tf_op jit(solution)/shard_map/pallas_call | solution.py:521
  88.1 1.0 %copy.9 = f32[64,16,2,128]{3,2,1,0:T(2,128)} copy(f32[64,16,2,128]{3,2,1,0:T(2,128)S(1)} %bitcast.2) | data formatting | bytes 2097152

commit v7 on v6

--- a/solution.py
+++ b/solution.py
@@ -377,9 +377,24 @@
                 lax.dot_general(values, expand[h, part], CONTRACT_ROWS, preferred_element_type=F32)
                 for part in range(2)], axis=0)
             lhs.append(jnp.where(mask, ex, 0.0).astype(BF))
-        for bx in range(4):
+        i = x * (1 - par) + z * par
+        c1, c2, c3 = (i + 1) % 4, (i + 2) % 4, (i + 3) % 4
+        minus, plus = copies(s, 0, ms1, mr1, par)
+
+        def send_minus():
+            ms1[s, 0, 0] = q[qs, c2, :, A, :].astype(BF)
+            ms1[s, 0, 1] = q[qs, c3, :, B, :].astype(BF)
+            minus.start()
+
+        def send_plus():
+            ms1[s, 1, 0] = q[qs, c2, :, B, :].astype(BF)
+            ms1[s, 1, 1] = q[qs, c1, :, A, :].astype(BF)
+            plus.start()
+
+        for bx in ((c2, c3, c1, i) if s == 0 else range(4)):
+            lanes = pl.ds(pl.multiple_of(256 * bx, 256), 256) if s == 0 else pl.ds(256 * bx, 256)
             pa, pb = [
-                jnp.dot(lhs[h], leg[h, tt, :, :, 256 * bx:256 * bx + 256].reshape(768, 256),
+                jnp.dot(lhs[h], leg[h, tt, :, :, lanes].reshape(768, 256),
                         preferred_element_type=F32)
                 for h in range(2)
             ]
@@ -390,15 +405,13 @@
                 second = jnp.where(low_lanes, pltpu.roll(a, 64, 1), b)
                 for bz, value in ((2 * half, first), (2 * half + 1, second)):
                     q[qs, bx * (1 - par) + bz * par, bz * (1 - par) + bx * par] = value
-        i = x * (1 - par) + z * par
-        c1, c2, c3 = (i + 1) % 4, (i + 2) % 4, (i + 3) % 4
-        minus, plus = copies(s, 0, ms1, mr1, par)
-        ms1[s, 0, 0] = q[qs, c2, :, A, :].astype(BF)
-        ms1[s, 0, 1] = q[qs, c3, :, B, :].astype(BF)
-        minus.start()
-        ms1[s, 1, 0] = q[qs, c2, :, B, :].astype(BF)
-        ms1[s, 1, 1] = q[qs, c1, :, A, :].astype(BF)
-        plus.start()
+            if s == 0 and bx is c3:
+                send_minus()
+            if s == 0 and bx is c1:
+                send_plus()
+        if s != 0:
+            send_minus()
+            send_plus()
 
     def relay1(s):
         par, qs = s % 2, s % 4

time: 89.3 us -> 89.3 us (level)
  no operation moved by 1% of the time
where the time goes in v7:
time: 89.3 us; the launch traced here: 89.1 us
  Pallas kernels  88.1 us (99%)
  local copies, waits for them, and re-layouts  0.97 us (1%)
    pallas_call x1, Pallas kernels, analysis(): pl.pallas_call(kernel, out_shape=pltpu.VMEM((2048, 128), F32), in_specs=[...  88.1 us

profile of v7, /device:TPU:0, one launch (start us, length us, event | category | flops | bytes accessed | tf_op | source)
XLA Modules:
  0.0 89.1 jit_solution(5288721457421208953)
XLA Ops:
  0.0 88.1 %shard_map.73 = f32[2048,128]{1,0:T(8,128)S(1)} custom-call(f32[16,64,512]{2,1,0:T(8,128)} %field_hbm.1, s32[64,512]{1,0:T(8,128)} %mask_hbm.1, s32[8,128]{1,0:T(8,128)} %bitcast.3, bf16[16,64,256]{2,1,0:T(8,128)(2,1)} %constant.6.clone.high_hbm, bf16[16,64,256]{2,1,0:T(8,128)(2,1)} %constant.7.clone.low_hbm, bf16[128,128]{1,0:T(8,128)(2,1)} %constant.8.clone.perm_hbm, ...), custom_call_target="tpu_custom_call" | custom-call | tf_op jit(solution)/shard_map/pallas_call | solution.py:534
  88.1 1.0 %copy.9 = f32[64,16,2,128]{3,2,1,0:T(2,128)} copy(f32[64,16,2,128]{3,2,1,0:T(2,128)S(1)} %bitcast.2) | data formatting | bytes 2097152
